TPU v7x, 512 devices: a whole 4x4x16 slice. The times are simulated.
512 devices in a mesh: lon: 8 (over x, core), lat: 16 (over z), lev: 4 (over y).
Axes of the slice: x: 4, y: 4, z: 16, core: 2. Of those that a mesh axis runs over, the one named last changes fastest.
Arguments:
- solution: float32 [36, 8, 128, 1024], P(None, 'lev', 'lat', 'lon'), may hold values from -6 to 6
- residual: float32 [36, 8, 128, 1024], P(None, 'lev', 'lat', 'lon'), may hold values from -24 to 24
- direction: float32 [36, 8, 128, 1024], P(None, 'lev', 'lat', 'lon'), may hold values from -24 to 24
- ensemble: bfloat16 [32, 4, 8, 128, 1024], P(None, None, 'lev', 'lat', 'lon'), may hold values from -6 to 6
- static_sd: float32 [4, 8, 128, 1024], P(None, 'lev', 'lat', 'lon'), may hold values from 0.5 to 2
- send_tile: int32 [4, 8, 16, 128, 2], P('lev', 'lon', 'lat'), may hold values from 0 to 15
- pair_count: int32 [4, 8, 16, 128], P('lev', 'lon', 'lat'), may hold values from 1 to 2, as said below
- obs_weight: bfloat16 [4, 8, 16, 128, 2, 8, 512], P('lev', 'lon', 'lat'), may hold values from -0.25 to 0.25
- obs_precision: float32 [4, 8, 16, 128, 2, 8], P('lev', 'lon', 'lat'), may hold values from 100 to 3000
Outputs:
- new_solution: float32 [36, 8, 128, 1024], P(None, 'lev', 'lat', 'lon')
- new_residual: float32 [36, 8, 128, 1024], P(None, 'lev', 'lat', 'lon')
- new_direction: float32 [36, 8, 128, 1024], P(None, 'lev', 'lat', 'lon')
Inputs may be any that keep to these rules, and one draw needn't show every extreme that they name: `pair_count`: every device sends at least one and at most 2 live slots to every owner of its level plane; in every level plane some owner has 2 live slots from every device of the plane.
All inputs are finite; a program needn't handle non-finite values.
Results may differ from a plain program's by a relative error of at most 0.0034.
Values may be sent and summed in bfloat16 or wider, within the bound.
No kernel may reach another device: no remote copies, remote signals or barrier semaphores. Data moves between devices by JAX's collectives and lax.ppermute only.
A program may use at most 64 MiB of HBM per device.

v0:
```python
import jax
import jax.numpy as jnp
from jax import lax
from jax.sharding import Mesh
from jax.sharding import PartitionSpec as P

LON_LAT_LEV = ("lon_0", "lon_1", "lat", "lev")
LON = ("lon_0", "lon_1")
LON_LAT = ("lon_0", "lon_1", "lat")


spread_lon = 0.075
spread_lat = 0.3
spread_lev = 0.075
ens_share = 0.75
static_part = 0.5


def with_halo(x, sides, width):
    edges = {}
    for axis, dim in sides:
        devices, length = (lax.axis_size(axis), x.shape[dim])
        up = [(i, (i + 1) % devices) for i in range(devices)]
        last = lax.slice_in_dim(x, length - width, length, axis=dim)
        initial = lax.slice_in_dim(x, 0, width, axis=dim)
        edges[dim] = (
            lax.ppermute(last, axis, up),
            lax.ppermute(initial, axis, [(b, a) for a, b in up]),
        )
    done = []
    for _, dim in sides:
        low, high = edges[dim]
        around = [(width, width) if d in done else (0, 0) for d in range(x.ndim)]
        x = jnp.concatenate([jnp.pad(low, around), x, jnp.pad(high, around)], axis=dim)
        done.append(dim)
    return x


def one_axis_at_a_time(x, axes):
    for axis in axes:
        x = lax.psum(x, axis)
    return x


def one_pass(padded):
    centre = padded[:, 1:-1, 1:-1, 1:-1]
    result = centre * (1.0 - 2.0 * (spread_lon + spread_lat + spread_lev))
    result = result + spread_lon * (padded[:, 1:-1, 1:-1, 2:] + padded[:, 1:-1, 1:-1, :-2])
    result = result + spread_lat * (padded[:, 1:-1, 2:, 1:-1] + padded[:, 1:-1, :-2, 1:-1])
    result = result + spread_lev * (padded[:, 2:, 1:-1, 1:-1] + padded[:, :-2, 1:-1, 1:-1])
    return result


def inside_mask(levels, lat_rows, margin):
    lev_first = lax.axis_index("lev") * levels - margin
    lat_first = lax.axis_index("lat") * lat_rows - margin
    lev_total = levels * lax.axis_size("lev")
    lat_total = lat_rows * lax.axis_size("lat")
    lev_where = lev_first + jnp.arange(levels + 2 * margin, dtype=jnp.int32)
    lat_where = lat_first + jnp.arange(lat_rows + 2 * margin, dtype=jnp.int32)
    lev_inside = (lev_where >= 0) & (lev_where < lev_total)
    lat_inside = (lat_where >= 0) & (lat_where < lat_total)
    return (lev_inside[:, None] & lat_inside[None, :]).astype(jnp.float32)[:, :, None]


def smooth(fields):
    levels, lat_rows = (fields.shape[1], fields.shape[2])
    inside = inside_mask(levels, lat_rows, 1)
    for pass_index in range(4):
        padded = with_halo(fields, ((LON, 3), ("lat", 2), ("lev", 1)), 1)
        fields = one_pass(padded * inside)
    return fields


def body(
    solution,
    residual,
    direction,
    ensemble,
    static_sd,
    send_tile,
    pair_count,
    obs_weight,
    obs_precision,
):
    members, variables, levels, lat_rows, lon_cells = ensemble.shape
    scale_ens = (ens_share / members) ** 0.5
    tile_width = variables * lon_cells
    tile_total = levels * lat_rows
    group_size = send_tile.shape[3]
    slot_count = send_tile.shape[4]
    obs_count = obs_weight.shape[5]
    smoothed = smooth(direction)
    ens_part = jnp.sum(ensemble * smoothed[:members, None], axis=0)
    increment = (scale_ens * ens_part + static_part * static_sd * smoothed[members:]).astype(
        jnp.bfloat16
    )
    tile_table = increment.transpose(1, 2, 0, 3).reshape(tile_total, tile_width)
    tile_pick = send_tile.reshape(group_size * slot_count)
    is_live = (
        jnp.arange(slot_count, dtype=jnp.int32)[None, :] < pair_count.reshape(group_size)[:, None]
    )
    outgoing = jnp.take(tile_table, tile_pick, axis=0)
    outgoing = jnp.where(
        is_live.reshape(group_size * slot_count)[:, None], outgoing, jnp.zeros_like(outgoing)
    )
    outgoing = outgoing.reshape(group_size, slot_count, tile_width)
    arrived = lax.all_to_all(outgoing, LON_LAT, split_axis=0, concat_axis=0, tiled=True)
    weights = obs_weight.reshape(group_size, slot_count, obs_count, tile_width)
    predicted = jnp.einsum("gsbc,gsc->gsb", weights, arrived, preferred_element_type=jnp.float32)
    weighted = (obs_precision.reshape(group_size, slot_count, obs_count) * predicted).astype(
        jnp.bfloat16
    )
    returned = jnp.einsum("gsbc,gsb->gsc", weights, weighted, preferred_element_type=jnp.float32)
    came_back = lax.all_to_all(returned, LON_LAT, split_axis=0, concat_axis=0, tiled=True)
    came_back = came_back.reshape(group_size * slot_count, tile_width)
    one_hot = (tile_pick[:, None] == jnp.arange(tile_total, dtype=jnp.int32)[None, :]).astype(
        jnp.float32
    )
    adj_tiles = jnp.dot(
        one_hot.T, came_back, precision=lax.Precision.HIGHEST, preferred_element_type=jnp.float32
    )
    adjoint = adj_tiles.reshape(levels, lat_rows, variables, lon_cells).transpose(2, 0, 1, 3)
    back_ens = scale_ens * jnp.sum(ensemble * adjoint[None], axis=1)
    back_static = static_part * static_sd * adjoint
    back = jnp.concatenate([back_ens, back_static], axis=0)
    image_field = direction + smooth(back)
    start_norm, curvature, crossed, squared = (
        one_axis_at_a_time(jnp.sum(residual * residual), LON_LAT_LEV),
        one_axis_at_a_time(jnp.sum(direction * image_field), LON_LAT_LEV),
        one_axis_at_a_time(jnp.sum(residual * image_field), LON_LAT_LEV),
        one_axis_at_a_time(jnp.sum(image_field * image_field), LON_LAT_LEV),
    )
    step_size = start_norm / curvature
    new_residual = residual - step_size * image_field
    next_norm = start_norm - 2.0 * step_size * crossed + step_size * step_size * squared
    new_solution = solution + step_size * direction
    new_direction = new_residual + next_norm / (start_norm + 1e-06) * direction
    return (new_solution, new_residual, new_direction)


def solution(mesh):
    split = Mesh(
        mesh.devices.reshape(4, 2, mesh.shape["lat"], mesh.shape["lev"]),
        ("lon_0", "lon_1", "lat", "lev"),
    )
    in_specs = (
        P(None, "lev", "lat", LON),
        P(None, "lev", "lat", LON),
        P(None, "lev", "lat", LON),
        P(None, None, "lev", "lat", LON),
        P(None, "lev", "lat", LON),
        P("lev", LON, "lat", None, None),
        P("lev", LON, "lat", None),
        P("lev", LON, "lat", None, None, None, None),
        P("lev", LON, "lat", None, None, None),
    )
    out_specs = (P(None, "lev", "lat", LON), P(None, "lev", "lat", LON), P(None, "lev", "lat", LON))
    return jax.shard_map(body, mesh=split, in_specs=in_specs, out_specs=out_specs, check_vma=False)
```

profile of v0, /device:TPU:8, one launch (start us, length us, event | category | flops | bytes accessed | tf_op | source)
XLA Modules:
  0.0 346.9 jit_solution(12706583132823470760)
XLA Ops:
  10.1 6.1 %collective-permute-start.5 = (f32[36,1,8,128]{3,2,0,1:T(8,128)}, f32[36,1,8,128]{3,2,0,1:T(8,128)}, u32[]{:S(2)}, u32[]{:S(2)}) collective-permute-start(f32[36,1,8,128]{3,2,0,1:T(8,128)} %get-tuple-element.80), channel_id=1, source_target_pairs={{1,0},{2,1},{3,2},{0,3},{5,4},{6,5},{7,6},{4,7},{9,8},{10,9},{11,1... | collective-permute-start | bytes 442376 | tf_op jit(solution)/shard_map/ppermute | solution.py:28
  20.7 7.6 %collective-permute-start.4 = (f32[36,2,1,128]{3,2,0,1:T(1,128)S(1)}, f32[36,2,1,128]{3,2,0,1:T(1,128)S(1)}, u32[]{:S(2)}, u32[]{:S(2)}) collective-permute-start(f32[36,2,1,128]{3,2,0,1:T(1,128)S(1)} %get-tuple-element.82), channel_id=1, source_target_pairs={{4,0},{8,4},{12,8},{16,12},{20,16},{24,20},{28,24},{32,28},{36,32}... | collective-permute-start | bytes 110600 | tf_op jit(solution)/shard_map/ppermute | solution.py:28
  42.0 5.4 %collective-permute-start.10 = (f32[36,2,1,128]{3,2,0,1:T(1,128)S(1)}, f32[36,2,1,128]{3,2,0,1:T(1,128)S(1)}, u32[]{:S(2)}, u32[]{:S(2)}) collective-permute-start(f32[36,2,1,128]{3,2,0,1:T(1,128)S(1)} %get-tuple-element.76), channel_id=1, source_target_pairs={{4,0},{8,4},{12,8},{16,12},{20,16},{24,20},{28,24},{32,28},{36,32}... | collective-permute-start | bytes 110600 | tf_op jit(solution)/shard_map/ppermute | solution.py:28
  49.4 5.1 %collective-permute-done.7 = f32[36,2,1,128]{3,2,0,1:T(1,128)S(1)} collective-permute-done((f32[36,2,1,128]{3,2,0,1:T(1,128)S(1)}, f32[36,2,1,128]{3,2,0,1:T(1,128)S(1)}, u32[]{:S(2)}, u32[]{:S(2)}) %collective-permute-start.7) | collective-permute-done | bytes 36896 | tf_op jit(solution)/shard_map/ppermute | solution.py:27
  67.6 5.1 %collective-permute-start.16 = (f32[36,2,1,128]{3,2,0,1:T(1,128)S(1)}, f32[36,2,1,128]{3,2,0,1:T(1,128)S(1)}, u32[]{:S(2)}, u32[]{:S(2)}) collective-permute-start(f32[36,2,1,128]{3,2,0,1:T(1,128)S(1)} %get-tuple-element.70), channel_id=1, source_target_pairs={{4,0},{8,4},{12,8},{16,12},{20,16},{24,20},{28,24},{32,28},{36,32}... | collective-permute-start | bytes 110600 | tf_op jit(solution)/shard_map/ppermute | solution.py:28
  89.8 5.4 %collective-permute-start.22 = (f32[36,2,1,128]{3,2,0,1:T(1,128)}, f32[36,2,1,128]{3,2,0,1:T(1,128)S(1)}, u32[]{:S(2)}, u32[]{:S(2)}) collective-permute-start(f32[36,2,1,128]{3,2,0,1:T(1,128)} %get-tuple-element.64), channel_id=1, source_target_pairs={{4,0},{8,4},{12,8},{16,12},{20,16},{24,20},{28,24},{32,28},{36,32}... | collective-permute-start | bytes 110600 | tf_op jit(solution)/shard_map/ppermute | solution.py:28
  102.4 33.4 %all_to_all.10 = bf16[128,2,512]{2,1,0:T(2,128)(2,1)S(1)} all-to-all(bf16[128,2,512]{2,1,0:T(2,128)(2,1)S(1)} %broadcast_select_fusion.1), channel_id=1, replica_groups=mesh['lon_0'=4,'lon_1'=2,'lat'=16,'lev'=4] {'lon_0','lon_1','lat'}, dimensions={0} | all-to-all | bytes 524288 | tf_op jit(solution)/shard_map/all_to_all | solution.py:108
  138.8 7.1 %all-to-all-start.1 = ((f32[128,2,512]{2,1,0:T(2,128)}), f32[128,2,512]{2,1,0:T(2,128)S(1)}, u32[]{:S(2)}, u32[]{:S(2)}) async-start(f32[128,2,512]{2,1,0:T(2,128)} %bitcast.48), calls=%async_computation.1 | async-start | bytes 1048576 | tf_op jit(solution)/shard_map/all_to_all | solution.py:115
  146.0 31.2 %all-to-all-done.1 = f32[128,2,512]{2,1,0:T(2,128)S(1)} async-done(((f32[128,2,512]{2,1,0:T(2,128)}), f32[128,2,512]{2,1,0:T(2,128)S(1)}, u32[]{:S(2)}, u32[]{:S(2)}) %all-to-all-start.1) | async-done | bytes 524320 | tf_op jit(solution)/shard_map/all_to_all | solution.py:115
  187.0 4.0 %collective-permute-start.25 = (f32[36,2,1,128]{3,2,0,1:T(1,128)S(1)}, f32[36,2,1,128]{3,2,0,1:T(1,128)S(1)}, u32[]{:S(2)}, u32[]{:S(2)}) collective-permute-start(f32[36,2,1,128]{3,2,0,1:T(1,128)S(1)} %get-tuple-element.57), channel_id=1, source_target_pairs={{0,4},{4,8},{8,12},{12,16},{16,20},{20,24},{24,28},{28,32},{32,36}... | collective-permute-start | bytes 110600 | tf_op jit(solution)/shard_map/ppermute | solution.py:27
  194.2 7.3 %collective-permute-done.26 = f32[36,2,8,1]{3,2,0,1:T(8,128)S(1)} collective-permute-done((f32[36,2,8,1]{3,2,0,1:T(8,128)S(1)}, f32[36,2,8,1]{3,2,0,1:T(8,128)S(1)}, u32[]{:S(2)}, u32[]{:S(2)}) %collective-permute-start.26) | collective-permute-done | bytes 2336 | tf_op jit(solution)/shard_map/ppermute | solution.py:27
  201.6 4.2 %collective-permute-done.27 = f32[36,2,8,1]{3,2,0,1:T(8,128)S(1)} collective-permute-done((f32[36,2,8,1]{3,2,0,1:T(8,128)S(1)}, f32[36,2,8,1]{3,2,0,1:T(8,128)S(1)}, u32[]{:S(2)}, u32[]{:S(2)}) %collective-permute-start.27) | collective-permute-done | bytes 2336 | tf_op jit(solution)/shard_map/ppermute | solution.py:28
  210.5 4.9 %collective-permute-start.35 = (f32[36,1,8,128]{3,2,0,1:T(8,128)S(1)}, f32[36,1,8,128]{3,2,0,1:T(8,128)S(1)}, u32[]{:S(2)}, u32[]{:S(2)}) collective-permute-start(f32[36,1,8,128]{3,2,0,1:T(8,128)S(1)} %get-tuple-element.50), channel_id=1, source_target_pairs={{1,0},{2,1},{3,2},{0,3},{5,4},{6,5},{7,6},{4,7},{9,8},{10,9},{11,1... | collective-permute-start | bytes 442376 | tf_op jit(solution)/shard_map/ppermute | solution.py:28
  222.7 7.3 %collective-permute-done.32 = f32[36,2,8,1]{3,2,0,1:T(8,128)S(1)} collective-permute-done((f32[36,2,8,1]{3,2,0,1:T(8,128)S(1)}, f32[36,2,8,1]{3,2,0,1:T(8,128)S(1)}, u32[]{:S(2)}, u32[]{:S(2)}) %collective-permute-start.32) | collective-permute-done | bytes 2336 | tf_op jit(solution)/shard_map/ppermute | solution.py:27
  230.0 4.2 %collective-permute-done.33 = f32[36,2,8,1]{3,2,0,1:T(8,128)S(1)} collective-permute-done((f32[36,2,8,1]{3,2,0,1:T(8,128)S(1)}, f32[36,2,8,1]{3,2,0,1:T(8,128)S(1)}, u32[]{:S(2)}, u32[]{:S(2)}) %collective-permute-start.33) | collective-permute-done | bytes 2336 | tf_op jit(solution)/shard_map/ppermute | solution.py:28
  238.3 5.1 %collective-permute-start.41 = (f32[36,1,8,128]{3,2,0,1:T(8,128)S(1)}, f32[36,1,8,128]{3,2,0,1:T(8,128)S(1)}, u32[]{:S(2)}, u32[]{:S(2)}) collective-permute-start(f32[36,1,8,128]{3,2,0,1:T(8,128)S(1)} %get-tuple-element.44), channel_id=1, source_target_pairs={{1,0},{2,1},{3,2},{0,3},{5,4},{6,5},{7,6},{4,7},{9,8},{10,9},{11,1... | collective-permute-start | bytes 442376 | tf_op jit(solution)/shard_map/ppermute | solution.py:28
  245.4 5.1 %collective-permute-start.40 = (f32[36,2,1,128]{3,2,0,1:T(1,128)S(1)}, f32[36,2,1,128]{3,2,0,1:T(1,128)S(1)}, u32[]{:S(2)}, u32[]{:S(2)}) collective-permute-start(f32[36,2,1,128]{3,2,0,1:T(1,128)S(1)} %get-tuple-element.46), channel_id=1, source_target_pairs={{4,0},{8,4},{12,8},{16,12},{20,16},{24,20},{28,24},{32,28},{36,32}... | collective-permute-start | bytes 110600 | tf_op jit(solution)/shard_map/ppermute | solution.py:28
  250.7 7.3 %collective-permute-done.38 = f32[36,2,8,1]{3,2,0,1:T(8,128)S(1)} collective-permute-done((f32[36,2,8,1]{3,2,0,1:T(8,128)S(1)}, f32[36,2,8,1]{3,2,0,1:T(8,128)S(1)}, u32[]{:S(2)}, u32[]{:S(2)}) %collective-permute-start.38) | collective-permute-done | bytes 2336 | tf_op jit(solution)/shard_map/ppermute | solution.py:27
  258.0 4.2 %collective-permute-done.39 = f32[36,2,8,1]{3,2,0,1:T(8,128)S(1)} collective-permute-done((f32[36,2,8,1]{3,2,0,1:T(8,128)S(1)}, f32[36,2,8,1]{3,2,0,1:T(8,128)S(1)}, u32[]{:S(2)}, u32[]{:S(2)}) %collective-permute-start.39) | collective-permute-done | bytes 2336 | tf_op jit(solution)/shard_map/ppermute | solution.py:28
  266.6 5.1 %collective-permute-start.47 = (f32[36,1,8,128]{3,2,0,1:T(8,128)S(1)}, f32[36,1,8,128]{3,2,0,1:T(8,128)S(1)}, u32[]{:S(2)}, u32[]{:S(2)}) collective-permute-start(f32[36,1,8,128]{3,2,0,1:T(8,128)S(1)} %get-tuple-element.38), channel_id=1, source_target_pairs={{1,0},{2,1},{3,2},{0,3},{5,4},{6,5},{7,6},{4,7},{9,8},{10,9},{11,1... | collective-permute-start | bytes 442376 | tf_op jit(solution)/shard_map/ppermute | solution.py:28
  276.6 5.1 %collective-permute-start.46 = (f32[36,2,1,128]{3,2,0,1:T(1,128)S(1)}, f32[36,2,1,128]{3,2,0,1:T(1,128)S(1)}, u32[]{:S(2)}, u32[]{:S(2)}) collective-permute-start(f32[36,2,1,128]{3,2,0,1:T(1,128)S(1)} %get-tuple-element.40), channel_id=1, source_target_pairs={{4,0},{8,4},{12,8},{16,12},{20,16},{24,20},{28,24},{32,28},{36,32}... | collective-permute-start | bytes 110600 | tf_op jit(solution)/shard_map/ppermute | solution.py:28
  286.0 8.9 %all-reduce.34 = (f32[]{:T(128)}, f32[]{:T(128)}, f32[]{:T(128)}, f32[]{:T(128)}) all-reduce(f32[]{:T(128)} %multiply_reduce_fusion.3, f32[]{:T(128)} %get-tuple-element.14, f32[]{:T(128)} %get-tuple-element.13, f32[]{:T(128)} %get-tuple-element.12), channel_id=1, replica_groups=mesh['lon_0'=4,'lon_1'=2,'lat'=16,'lev'=4] {'lon_0'}, use_global_device_ids=true, to_apply=%region_1.2 | all-reduce | flops 4 | bytes 32 | tf_op jit(solution)/shard_map/psum | solution.py:41
  298.0 31.2 %all-reduce.32 = (f32[]{:T(128)}, f32[]{:T(128)}, f32[]{:T(128)}, f32[]{:T(128)}) all-reduce(f32[]{:T(128)} %get-tuple-element.27, f32[]{:T(128)} %get-tuple-element.28, f32[]{:T(128)} %get-tuple-element.29, f32[]{:T(128)} %get-tuple-element.30), channel_id=1, replica_groups=mesh['lon_0'=4,'lon_1'=2,'lat'=16,'lev'=4] {'lat'}, use_global_device_ids=true, to_apply=%region_3.4 | all-reduce | flops 4 | bytes 32 | tf_op jit(solution)/shard_map/psum | solution.py:41
  329.2 11.6 %all-reduce.33 = (f32[]{:T(128)}, f32[]{:T(128)}, f32[]{:T(128)}, f32[]{:T(128)}) all-reduce(f32[]{:T(128)} %get-tuple-element.15, f32[]{:T(128)} %get-tuple-element.16, f32[]{:T(128)} %get-tuple-element.17, f32[]{:T(128)} %get-tuple-element.18), channel_id=1, replica_groups=mesh['lon_0'=4,'lon_1'=2,'lat'=16,'lev'=4] {'lev'}, use_global_device_ids=true, to_apply=%region_4.5 | all-reduce | flops 4 | bytes 32 | tf_op jit(solution)/shard_map/psum | solution.py:41
  (170 shorter events, 119.1 us)
Async XLA Ops:
  2.0 18.7 %collective-permute-start.2 = (f32[36,2,8,1]{3,2,0,1:T(8,128)S(1)}, f32[36,2,8,1]{3,2,0,1:T(8,128)S(1)}, u32[]{:S(2)}, u32[]{:S(2)}) collective-permute-start(f32[36,2,8,1]{3,2,0,1:T(8,128)S(1)} %get-tuple-element.77), channel_id=1, source_target_pairs={{0,64},{64,128},{128,192},{192,256},{256,320},{320,384},{384,448},... | collective-permute-start | bytes 6920 | tf_op jit(solution)/shard_map/ppermute | solution.py:27
  2.0 27.3 %collective-permute-start.3 = (f32[36,2,8,1]{3,2,0,1:T(8,128)S(1)}, f32[36,2,8,1]{3,2,0,1:T(8,128)S(1)}, u32[]{:S(2)}, u32[]{:S(2)}) collective-permute-start(f32[36,2,8,1]{3,2,0,1:T(8,128)S(1)} %get-tuple-element.78), channel_id=1, source_target_pairs={{64,0},{128,64},{192,128},{256,192},{320,256},{384,320},{448,384},... | collective-permute-start | bytes 6920 | tf_op jit(solution)/shard_map/ppermute | solution.py:28
  6.7 23.3 %collective-permute-start = (f32[36,1,8,128]{3,2,0,1:T(8,128)}, f32[36,1,8,128]{3,2,0,1:T(8,128)S(1)}, u32[]{:S(2)}, u32[]{:S(2)}) collective-permute-start(f32[36,1,8,128]{3,2,0,1:T(8,128)} %get-tuple-element.79), channel_id=1, source_target_pairs={{0,1},{1,2},{2,3},{3,0},{4,5},{5,6},{6,7},{7,4},{8,9},{9,10},{10,1... | collective-permute-start | bytes 442376 | tf_op jit(solution)/shard_map/ppermute | solution.py:27
  10.1 19.8 %collective-permute-start.5 = (f32[36,1,8,128]{3,2,0,1:T(8,128)}, f32[36,1,8,128]{3,2,0,1:T(8,128)}, u32[]{:S(2)}, u32[]{:S(2)}) collective-permute-start(f32[36,1,8,128]{3,2,0,1:T(8,128)} %get-tuple-element.80), channel_id=1, source_target_pairs={{1,0},{2,1},{3,2},{0,3},{5,4},{6,5},{7,6},{4,7},{9,8},{10,9},{11,1... | collective-permute-start | bytes 442376 | tf_op jit(solution)/shard_map/ppermute | solution.py:28
  33.2 16.2 %collective-permute-start.9 = (f32[36,2,8,1]{3,2,0,1:T(8,128)S(1)}, f32[36,2,8,1]{3,2,0,1:T(8,128)S(1)}, u32[]{:S(2)}, u32[]{:S(2)}) collective-permute-start(f32[36,2,8,1]{3,2,0,1:T(8,128)S(1)} %get-tuple-element.72), channel_id=1, source_target_pairs={{64,0},{128,64},{192,128},{256,192},{320,256},{384,320},{448,384},... | collective-permute-start | bytes 6920 | tf_op jit(solution)/shard_map/ppermute | solution.py:28
  36.2 18.4 %collective-permute-start.11 = (f32[36,1,8,128]{3,2,0,1:T(8,128)S(1)}, f32[36,1,8,128]{3,2,0,1:T(8,128)S(1)}, u32[]{:S(2)}, u32[]{:S(2)}) collective-permute-start(f32[36,1,8,128]{3,2,0,1:T(8,128)S(1)} %get-tuple-element.74), channel_id=1, source_target_pairs={{1,0},{2,1},{3,2},{0,3},{5,4},{6,5},{7,6},{4,7},{9,8},{10,9},{11,1... | collective-permute-start | bytes 442376 | tf_op jit(solution)/shard_map/ppermute | solution.py:28
  39.7 14.8 %collective-permute-start.6 = (f32[36,1,8,128]{3,2,0,1:T(8,128)S(1)}, f32[36,1,8,128]{3,2,0,1:T(8,128)S(1)}, u32[]{:S(2)}, u32[]{:S(2)}) collective-permute-start(f32[36,1,8,128]{3,2,0,1:T(8,128)S(1)} %get-tuple-element.73), channel_id=1, source_target_pairs={{0,1},{1,2},{2,3},{3,0},{4,5},{5,6},{6,7},{7,4},{8,9},{9,10},{10,1... | collective-permute-start | bytes 442376 | tf_op jit(solution)/shard_map/ppermute | solution.py:27
  56.8 15.9 %collective-permute-start.15 = (f32[36,2,8,1]{3,2,0,1:T(8,128)S(1)}, f32[36,2,8,1]{3,2,0,1:T(8,128)S(1)}, u32[]{:S(2)}, u32[]{:S(2)}) collective-permute-start(f32[36,2,8,1]{3,2,0,1:T(8,128)S(1)} %get-tuple-element.66), channel_id=1, source_target_pairs={{64,0},{128,64},{192,128},{256,192},{320,256},{384,320},{448,384},... | collective-permute-start | bytes 6920 | tf_op jit(solution)/shard_map/ppermute | solution.py:28
  77.9 19.4 %collective-permute-start.18 = (f32[36,1,8,128]{3,2,0,1:T(8,128)}, f32[36,1,8,128]{3,2,0,1:T(8,128)S(1)}, u32[]{:S(2)}, u32[]{:S(2)}) collective-permute-start(f32[36,1,8,128]{3,2,0,1:T(8,128)} %get-tuple-element.61), channel_id=1, source_target_pairs={{0,1},{1,2},{2,3},{3,0},{4,5},{5,6},{6,7},{7,4},{8,9},{9,10},{10,1... | collective-permute-start | bytes 442376 | tf_op jit(solution)/shard_map/ppermute | solution.py:27
  81.8 15.4 %collective-permute-start.23 = (f32[36,1,8,128]{3,2,0,1:T(8,128)}, f32[36,1,8,128]{3,2,0,1:T(8,128)}, u32[]{:S(2)}, u32[]{:S(2)}) collective-permute-start(f32[36,1,8,128]{3,2,0,1:T(8,128)} %get-tuple-element.62), channel_id=1, source_target_pairs={{1,0},{2,1},{3,2},{0,3},{5,4},{6,5},{7,6},{4,7},{9,8},{10,9},{11,1... | collective-permute-start | bytes 442376 | tf_op jit(solution)/shard_map/ppermute | solution.py:28
  138.8 38.4 %all-to-all-start.1 = ((f32[128,2,512]{2,1,0:T(2,128)}), f32[128,2,512]{2,1,0:T(2,128)S(1)}, u32[]{:S(2)}, u32[]{:S(2)}) async-start(f32[128,2,512]{2,1,0:T(2,128)} %bitcast.48), calls=%async_computation.1 | async-start | bytes 1048576 | tf_op jit(solution)/shard_map/all_to_all | solution.py:115
  180.1 25.7 %collective-permute-start.24 = (f32[36,1,8,128]{3,2,0,1:T(8,128)S(1)}, f32[36,1,8,128]{3,2,0,1:T(8,128)S(1)}, u32[]{:S(2)}, u32[]{:S(2)}) collective-permute-start(f32[36,1,8,128]{3,2,0,1:T(8,128)S(1)} %get-tuple-element.55), channel_id=1, source_target_pairs={{0,1},{1,2},{2,3},{3,0},{4,5},{5,6},{6,7},{7,4},{8,9},{9,10},{10,1... | collective-permute-start | bytes 442376 | tf_op jit(solution)/shard_map/ppermute | solution.py:27
  183.3 22.6 %collective-permute-start.29 = (f32[36,1,8,128]{3,2,0,1:T(8,128)S(1)}, f32[36,1,8,128]{3,2,0,1:T(8,128)S(1)}, u32[]{:S(2)}, u32[]{:S(2)}) collective-permute-start(f32[36,1,8,128]{3,2,0,1:T(8,128)S(1)} %get-tuple-element.56), channel_id=1, source_target_pairs={{1,0},{2,1},{3,2},{0,3},{5,4},{6,5},{7,6},{4,7},{9,8},{10,9},{11,1... | collective-permute-start | bytes 442376 | tf_op jit(solution)/shard_map/ppermute | solution.py:28
  187.0 18.8 %collective-permute-start.25 = (f32[36,2,1,128]{3,2,0,1:T(1,128)S(1)}, f32[36,2,1,128]{3,2,0,1:T(1,128)S(1)}, u32[]{:S(2)}, u32[]{:S(2)}) collective-permute-start(f32[36,2,1,128]{3,2,0,1:T(1,128)S(1)} %get-tuple-element.57), channel_id=1, source_target_pairs={{0,4},{4,8},{8,12},{12,16},{16,20},{20,24},{24,28},{28,32},{32,36}... | collective-permute-start | bytes 110600 | tf_op jit(solution)/shard_map/ppermute | solution.py:27
  208.3 25.9 %collective-permute-start.30 = (f32[36,1,8,128]{3,2,0,1:T(8,128)S(1)}, f32[36,1,8,128]{3,2,0,1:T(8,128)S(1)}, u32[]{:S(2)}, u32[]{:S(2)}) collective-permute-start(f32[36,1,8,128]{3,2,0,1:T(8,128)S(1)} %get-tuple-element.49), channel_id=1, source_target_pairs={{0,1},{1,2},{2,3},{3,0},{4,5},{5,6},{6,7},{7,4},{8,9},{9,10},{10,1... | collective-permute-start | bytes 442376 | tf_op jit(solution)/shard_map/ppermute | solution.py:27
  210.5 23.7 %collective-permute-start.35 = (f32[36,1,8,128]{3,2,0,1:T(8,128)S(1)}, f32[36,1,8,128]{3,2,0,1:T(8,128)S(1)}, u32[]{:S(2)}, u32[]{:S(2)}) collective-permute-start(f32[36,1,8,128]{3,2,0,1:T(8,128)S(1)} %get-tuple-element.50), channel_id=1, source_target_pairs={{1,0},{2,1},{3,2},{0,3},{5,4},{6,5},{7,6},{4,7},{9,8},{10,9},{11,1... | collective-permute-start | bytes 442376 | tf_op jit(solution)/shard_map/ppermute | solution.py:28
  215.4 18.8 %collective-permute-start.31 = (f32[36,2,1,128]{3,2,0,1:T(1,128)S(1)}, f32[36,2,1,128]{3,2,0,1:T(1,128)S(1)}, u32[]{:S(2)}, u32[]{:S(2)}) collective-permute-start(f32[36,2,1,128]{3,2,0,1:T(1,128)S(1)} %get-tuple-element.51), channel_id=1, source_target_pairs={{0,4},{4,8},{8,12},{12,16},{16,20},{20,24},{24,28},{28,32},{32,36}... | collective-permute-start | bytes 110600 | tf_op jit(solution)/shard_map/ppermute | solution.py:27
  218.5 15.7 %collective-permute-start.34 = (f32[36,2,1,128]{3,2,0,1:T(1,128)S(1)}, f32[36,2,1,128]{3,2,0,1:T(1,128)S(1)}, u32[]{:S(2)}, u32[]{:S(2)}) collective-permute-start(f32[36,2,1,128]{3,2,0,1:T(1,128)S(1)} %get-tuple-element.52), channel_id=1, source_target_pairs={{4,0},{8,4},{12,8},{16,12},{20,16},{24,20},{28,24},{32,28},{36,32}... | collective-permute-start | bytes 110600 | tf_op jit(solution)/shard_map/ppermute | solution.py:28
  236.4 25.9 %collective-permute-start.36 = (f32[36,1,8,128]{3,2,0,1:T(8,128)S(1)}, f32[36,1,8,128]{3,2,0,1:T(8,128)S(1)}, u32[]{:S(2)}, u32[]{:S(2)}) collective-permute-start(f32[36,1,8,128]{3,2,0,1:T(8,128)S(1)} %get-tuple-element.43), channel_id=1, source_target_pairs={{0,1},{1,2},{2,3},{3,0},{4,5},{5,6},{6,7},{7,4},{8,9},{9,10},{10,1... | collective-permute-start | bytes 442376 | tf_op jit(solution)/shard_map/ppermute | solution.py:27
  238.3 24.0 %collective-permute-start.41 = (f32[36,1,8,128]{3,2,0,1:T(8,128)S(1)}, f32[36,1,8,128]{3,2,0,1:T(8,128)S(1)}, u32[]{:S(2)}, u32[]{:S(2)}) collective-permute-start(f32[36,1,8,128]{3,2,0,1:T(8,128)S(1)} %get-tuple-element.44), channel_id=1, source_target_pairs={{1,0},{2,1},{3,2},{0,3},{5,4},{6,5},{7,6},{4,7},{9,8},{10,9},{11,1... | collective-permute-start | bytes 442376 | tf_op jit(solution)/shard_map/ppermute | solution.py:28
  243.5 18.8 %collective-permute-start.37 = (f32[36,2,1,128]{3,2,0,1:T(1,128)S(1)}, f32[36,2,1,128]{3,2,0,1:T(1,128)S(1)}, u32[]{:S(2)}, u32[]{:S(2)}) collective-permute-start(f32[36,2,1,128]{3,2,0,1:T(1,128)S(1)} %get-tuple-element.45), channel_id=1, source_target_pairs={{0,4},{4,8},{8,12},{12,16},{16,20},{20,24},{24,28},{28,32},{32,36}... | collective-permute-start | bytes 110600 | tf_op jit(solution)/shard_map/ppermute | solution.py:27
  245.4 16.9 %collective-permute-start.40 = (f32[36,2,1,128]{3,2,0,1:T(1,128)S(1)}, f32[36,2,1,128]{3,2,0,1:T(1,128)S(1)}, u32[]{:S(2)}, u32[]{:S(2)}) collective-permute-start(f32[36,2,1,128]{3,2,0,1:T(1,128)S(1)} %get-tuple-element.46), channel_id=1, source_target_pairs={{4,0},{8,4},{12,8},{16,12},{20,16},{24,20},{28,24},{32,28},{36,32}... | collective-permute-start | bytes 110600 | tf_op jit(solution)/shard_map/ppermute | solution.py:28
  264.6 18.8 %collective-permute-start.42 = (f32[36,1,8,128]{3,2,0,1:T(8,128)S(1)}, f32[36,1,8,128]{3,2,0,1:T(8,128)S(1)}, u32[]{:S(2)}, u32[]{:S(2)}) collective-permute-start(f32[36,1,8,128]{3,2,0,1:T(8,128)S(1)} %get-tuple-element.37), channel_id=1, source_target_pairs={{0,1},{1,2},{2,3},{3,0},{4,5},{5,6},{6,7},{7,4},{8,9},{9,10},{10,1... | collective-permute-start | bytes 442376 | tf_op jit(solution)/shard_map/ppermute | solution.py:27
  266.6 16.7 %collective-permute-start.47 = (f32[36,1,8,128]{3,2,0,1:T(8,128)S(1)}, f32[36,1,8,128]{3,2,0,1:T(8,128)S(1)}, u32[]{:S(2)}, u32[]{:S(2)}) collective-permute-start(f32[36,1,8,128]{3,2,0,1:T(8,128)S(1)} %get-tuple-element.38), channel_id=1, source_target_pairs={{1,0},{2,1},{3,2},{0,3},{5,4},{6,5},{7,6},{4,7},{9,8},{10,9},{11,1... | collective-permute-start | bytes 442376 | tf_op jit(solution)/shard_map/ppermute | solution.py:28
  (34 other events, 482.1 us)
where the time goes:
time: 348 us; the launch traced here: 347 us
  starting transfers between devices  137 us (39%)
  blocking collectives  88.1 us (25%)
  waiting for transfers between devices  75.4 us (22%)
  other arithmetic  21.8 us (6%)
  local copies, waits for them, and re-layouts  17.1 us (5%)
  between operations  5.42 us (2%)
    ppermute x24, starting transfers between devices, with_halo(): lax.ppermute(initial, axis, [(b, a) for a, b in up])  88.8 us
    psum x4, blocking collectives, one_axis_at_a_time(): x = lax.psum(x, axis)  54.7 us
    ppermute x24, starting transfers between devices, with_halo(): lax.ppermute(last, axis, up)  41.2 us
    all_to_all x1, blocking collectives, body(): lax.all_to_all(outgoing, LON_LAT, split_axis=0, concat_axis=0, tiled=True)  33.4 us
    all_to_all x1, waiting for transfers between devices, body(): lax.all_to_all(returned, LON_LAT, split_axis=0, concat_axis=0, tiled=True)  31.2 us
    ppermute x24, waiting for transfers between devices, with_halo(): lax.ppermute(last, axis, up)  27.2 us
    ppermute x24, waiting for transfers between devices, with_halo(): lax.ppermute(initial, axis, [(b, a) for a, b in up])  17 us
    mul x8, other arithmetic, smooth(): fields = one_pass(padded * inside)  14.2 us
  transfers between devices with their start and end apart: 49, of which 12 were waited for; matrix products, arithmetic and copies ran while one was open for 2% of the time, Pallas kernels for 0%

commit v1 on v0

v1 whole, which is shorter than its diff:
```python
import jax
import jax.numpy as jnp
from jax import lax
from jax.experimental import pallas as pl
from jax.experimental.pallas import tpu as pltpu
from jax.sharding import Mesh
from jax.sharding import PartitionSpec as P

LON = ("lon_0", "lon_1")
LON_LAT = ("lon_0", "lon_1", "lat")


spread_lon = 0.075
spread_lat = 0.3
spread_lev = 0.075
ens_share = 0.75
static_part = 0.5
HALO = 4
VMEM_BYTES = 12 * 1024 * 1024


def shift(x, axis, step):
    devices = lax.axis_size(axis)
    return lax.ppermute(x, axis, [(i, (i + step) % devices) for i in range(devices)])


def total_over(row, axes):
    copies = lax.axis_size(axes)
    rows = jnp.broadcast_to(row[None, :], (copies, row.shape[0]))
    rows = lax.all_to_all(rows, axes, split_axis=0, concat_axis=0, tiled=True)
    return jnp.sum(rows, axis=0)


def pack_kernel(own_ref, north_ref, south_ref, full_ref, first_ref, last_ref):
    groups, fields, planes = own_ref.shape[:3]
    row = lax.broadcasted_iota(jnp.int32, (8, 128), 0)

    def one_field(f, carry):
        rows = []
        for q in range(groups):
            north = north_ref[q, f]
            south = south_ref[q, f]
            for j in range(planes):
                own = pltpu.roll(own_ref[q, f, j], 4, 0)
                above = north if j == 0 else pltpu.roll(north, 4, 0)
                below = pltpu.roll(south, 4, 0) if j == 0 else south
                top = jnp.where(row < 4, above, own)
                bottom = jnp.where(row < 4, own, below)
                full_ref[q, f, j, 0:8] = top
                full_ref[q, f, j, 8:16] = bottom
                rows += [top, bottom]
        columns = jnp.concatenate(rows, axis=0).T
        first_ref[f] = columns[0:8]
        last_ref[f] = columns[120:128]
        return carry

    lax.fori_loop(0, fields, one_field, 0)


def smooth_kernel(place_ref, full_ref, west_ref, east_ref, out_ref):
    groups, fields, planes = full_ref.shape[:3]
    total = groups * planes * 16
    lane = lax.broadcasted_iota(jnp.int32, (total, 128), 1)
    row = lax.broadcasted_iota(jnp.int32, (total, 128), 0) % 16
    sub = lax.broadcasted_iota(jnp.int32, (8, 128), 0)
    low = jnp.where(place_ref[0] == 0, HALO, 0)
    high = jnp.where(place_ref[0] == place_ref[1] - 1, 16 - HALO, 16)
    inside = jnp.where((row >= low) & (row < high), 1.0, 0.0).astype(jnp.float32)
    left_edge = lane == 0
    right_edge = lane == 127
    centre = 1.0 - 2.0 * (spread_lon + spread_lat + spread_lev)
    blank = jnp.zeros((16, 128), jnp.float32)

    def combine(x, beside):
        across = pltpu.roll(x, 1, 0) + pltpu.roll(x, total - 1, 0)
        above = jnp.concatenate([x[16:], blank], axis=0)
        below = jnp.concatenate([blank, x[: total - 16]], axis=0)
        result = centre * x + spread_lon * beside
        result = result + spread_lat * across
        result = result + spread_lev * (above + below)
        return result * inside

    def one_field(f, carry):
        x = full_ref[:, f].reshape(total, 128) * inside
        outer = jnp.concatenate(
            [east_ref[f], jnp.zeros((112, 128), jnp.float32), west_ref[f]], axis=0
        ).T * inside
        for _ in range(4):
            x_left, outer_left = pltpu.roll(x, 1, 1), pltpu.roll(outer, 1, 1)
            x_right, outer_right = pltpu.roll(x, 127, 1), pltpu.roll(outer, 127, 1)
            beside = jnp.where(left_edge, outer_left, x_left) + jnp.where(
                right_edge, outer_right, x_right
            )
            outer_beside = jnp.where(left_edge, x_left, outer_left) + jnp.where(
                right_edge, x_right, outer_right
            )
            x, outer = combine(x, beside), combine(outer, outer_beside)
        for q in range(groups):
            for j in range(planes):
                start = (q * planes + j) * 16
                top = pltpu.roll(x[start : start + 8], 4, 0)
                bottom = pltpu.roll(x[start + 8 : start + 16], 4, 0)
                out_ref[q, f, j] = jnp.where(sub < 4, top, bottom)
        return carry

    lax.fori_loop(0, fields, one_field, 0)


def smooth(fields):
    count, levels, lat_rows, lon_cells = fields.shape
    groups = lax.axis_size("lev")
    share = count // groups
    blocks = fields.reshape(groups, share, levels, lat_rows, lon_cells)
    blocks = lax.all_to_all(blocks, "lev", split_axis=0, concat_axis=0, tiled=True)
    halo_shape = (groups, share, levels * HALO, lon_cells)
    north = shift(blocks[..., lat_rows - HALO :, :].reshape(halo_shape), "lat", 1)
    south = shift(blocks[..., :HALO, :].reshape(halo_shape), "lat", -1)
    strip = jax.ShapeDtypeStruct((share, 8, 128), jnp.float32)
    full, first, last = pl.pallas_call(
        pack_kernel,
        out_shape=(
            jax.ShapeDtypeStruct((groups, share, levels, 16, lon_cells), jnp.float32),
            strip,
            strip,
        ),
        compiler_params=pltpu.CompilerParams(vmem_limit_bytes=VMEM_BYTES),
        name="pack",
    )(blocks, north, south)
    west = shift(last, LON, 1)
    east = shift(first, LON, -1)
    place = jnp.stack([lax.axis_index("lat"), lax.axis_size("lat")]).astype(jnp.int32)
    blocks = pl.pallas_call(
        smooth_kernel,
        out_shape=jax.ShapeDtypeStruct(blocks.shape, jnp.float32),
        in_specs=[pl.BlockSpec(memory_space=pltpu.SMEM)]
        + [pl.BlockSpec(memory_space=pltpu.VMEM)] * 3,
        out_specs=pl.BlockSpec(memory_space=pltpu.VMEM),
        compiler_params=pltpu.CompilerParams(vmem_limit_bytes=VMEM_BYTES),
        name="smooth",
    )(place, full, west, east)
    blocks = lax.all_to_all(blocks, "lev", split_axis=0, concat_axis=0, tiled=True)
    return blocks.reshape(fields.shape)


def body(
    solution,
    residual,
    direction,
    ensemble,
    static_sd,
    send_tile,
    pair_count,
    obs_weight,
    obs_precision,
):
    members, variables, levels, lat_rows, lon_cells = ensemble.shape
    scale_ens = (ens_share / members) ** 0.5
    tile_width = variables * lon_cells
    tile_total = levels * lat_rows
    group_size = send_tile.shape[3]
    slot_count = send_tile.shape[4]
    obs_count = obs_weight.shape[5]
    smoothed = smooth(direction)
    ens_part = jnp.sum(ensemble * smoothed[:members, None], axis=0)
    increment = (scale_ens * ens_part + static_part * static_sd * smoothed[members:]).astype(
        jnp.bfloat16
    )
    tile_table = increment.transpose(1, 2, 0, 3).reshape(tile_total, tile_width)
    tile_pick = send_tile.reshape(group_size * slot_count)
    is_live = (
        jnp.arange(slot_count, dtype=jnp.int32)[None, :] < pair_count.reshape(group_size)[:, None]
    )
    outgoing = jnp.take(tile_table, tile_pick, axis=0)
    outgoing = jnp.where(
        is_live.reshape(group_size * slot_count)[:, None], outgoing, jnp.zeros_like(outgoing)
    )
    outgoing = outgoing.reshape(group_size, slot_count, tile_width)
    arrived = lax.all_to_all(outgoing, LON_LAT, split_axis=0, concat_axis=0, tiled=True)
    weights = obs_weight.reshape(group_size, slot_count, obs_count, tile_width)
    predicted = jnp.einsum("gsbc,gsc->gsb", weights, arrived, preferred_element_type=jnp.float32)
    weighted = (obs_precision.reshape(group_size, slot_count, obs_count) * predicted).astype(
        jnp.bfloat16
    )
    returned = jnp.einsum("gsbc,gsb->gsc", weights, weighted, preferred_element_type=jnp.float32)
    returned = returned.astype(jnp.bfloat16)
    came_back = lax.all_to_all(returned, LON_LAT, split_axis=0, concat_axis=0, tiled=True)
    came_back = came_back.reshape(group_size * slot_count, tile_width)
    one_hot = (tile_pick[:, None] == jnp.arange(tile_total, dtype=jnp.int32)[None, :]).astype(
        jnp.bfloat16
    )
    adj_tiles = jnp.dot(one_hot.T, came_back, preferred_element_type=jnp.float32)
    adjoint = adj_tiles.reshape(levels, lat_rows, variables, lon_cells).transpose(2, 0, 1, 3)
    back_ens = scale_ens * jnp.sum(ensemble * adjoint[None], axis=1)
    back_static = static_part * static_sd * adjoint
    back = jnp.concatenate([back_ens, back_static], axis=0)
    image_field = direction + smooth(back)
    sums = jnp.stack(
        [
            jnp.sum(residual * residual),
            jnp.sum(direction * image_field),
            jnp.sum(residual * image_field),
            jnp.sum(image_field * image_field),
        ]
    )
    sums = total_over(total_over(jnp.pad(sums, (0, 124)), ("lat", "lev")), LON)
    start_norm, curvature, crossed, squared = sums[0], sums[1], sums[2], sums[3]
    step_size = start_norm / curvature
    new_residual = residual - step_size * image_field
    next_norm = start_norm - 2.0 * step_size * crossed + step_size * step_size * squared
    new_solution = solution + step_size * direction
    new_direction = new_residual + next_norm / (start_norm + 1e-06) * direction
    return (new_solution, new_residual, new_direction)


def solution(mesh):
    split = Mesh(
        mesh.devices.reshape(4, 2, mesh.shape["lat"], mesh.shape["lev"]),
        ("lon_0", "lon_1", "lat", "lev"),
    )
    in_specs = (
        P(None, "lev", "lat", LON),
        P(None, "lev", "lat", LON),
        P(None, "lev", "lat", LON),
        P(None, None, "lev", "lat", LON),
        P(None, "lev", "lat", LON),
        P("lev", LON, "lat", None, None),
        P("lev", LON, "lat", None),
        P("lev", LON, "lat", None, None, None, None),
        P("lev", LON, "lat", None, None, None),
    )
    out_specs = (P(None, "lev", "lat", LON), P(None, "lev", "lat", LON), P(None, "lev", "lat", LON))
    return jax.shard_map(body, mesh=split, in_specs=in_specs, out_specs=out_specs, check_vma=False)
```

time: 348 us -> 203 us (0.58)
  the two profiles are of different devices: /device:TPU:8 before, /device:TPU:1 now
where the time goes in v1:
time: 203 us; the launch traced here: 202 us
  blocking collectives  85.6 us (42%)
  waiting for transfers between devices  45.3 us (22%)
  starting transfers between devices  39.8 us (20%)
  Pallas kernels  12.3 us (6%)
  other arithmetic  7.36 us (4%)
  between operations  5.03 us (2%)
  local copies, waits for them, and re-layouts  4.7 us (2%)
    all_to_all x1, blocking collectives, body(): lax.all_to_all(outgoing, LON_LAT, split_axis=0, concat_axis=0, tiled=True)  36.5 us
    all_to_all x2, blocking collectives, total_over(): rows = lax.all_to_all(rows, axes, split_axis=0, concat_axis=0, tiled=True)  30.6 us
    ppermute x8, starting transfers between devices, shift(): lax.ppermute(x, axis, [(i, (i + step) % devices) for i in range(devices)])  25.5 us
    all_to_all x1, waiting for transfers between devices, body(): lax.all_to_all(returned, LON_LAT, split_axis=0, concat_axis=0, tiled=True)  22.9 us
    all_to_all x2, blocking collectives, smooth(): lax.all_to_all(blocks, 'lev', split_axis=0, concat_axis=0, tiled=True)  18.4 us
    all_to_all x2, waiting for transfers between devices, smooth(): lax.all_to_all(blocks, 'lev', split_axis=0, concat_axis=0, tiled=True)  11.6 us
    ppermute x8, waiting for transfers between devices, shift(): lax.ppermute(x, axis, [(i, (i + step) % devices) for i in range(devices)])  10.7 us
    pallas_call x2, Pallas kernels, smooth(): pl.pallas_call(smooth_kernel, out_shape=jax.ShapeDtypeStruct(blocks.shape...  10.6 us
  transfers between devices with their start and end apart: 11, of which 10 were waited for; matrix products, arithmetic and copies ran while one was open for 1% of the time, Pallas kernels for 0%

profile of v1, /device:TPU:1, one launch (start us, length us, event | category | flops | bytes accessed | tf_op | source)
XLA Modules:
  0.0 202.0 jit_solution(5745450040835952476)
XLA Ops:
  0.7 5.1 %all-to-all-start = ((f32[4,9,2,8,128]{4,3,2,1,0:T(8,128)}), f32[4,9,2,8,128]{4,3,2,1,0:T(8,128)S(1)}, u32[]{:S(2)}, u32[]{:S(2)}) async-start(f32[4,9,2,8,128]{4,3,2,1,0:T(8,128)} %bitcast.77), calls=%async_computation | async-start | bytes 589824 | tf_op jit(solution)/shard_map/all_to_all | solution.py:114
  6.7 4.8 %all-to-all-done.own_ref = f32[4,9,2,8,128]{4,3,2,1,0:T(8,128)S(1)} async-done(((f32[4,9,2,8,128]{4,3,2,1,0:T(8,128)}), f32[4,9,2,8,128]{4,3,2,1,0:T(8,128)S(1)}, u32[]{:S(2)}, u32[]{:S(2)}) %all-to-all-start) | async-done | bytes 294944 | tf_op jit(solution)/shard_map/all_to_all | solution.py:114
  11.6 3.7 %collective-permute-start = (f32[4,9,8,128]{3,2,1,0:T(8,128)S(1)}, f32[4,9,8,128]{3,2,1,0:T(8,128)S(1)}, u32[]{:S(2)}, u32[]{:S(2)}) collective-permute-start(f32[4,9,8,128]{3,2,1,0:T(8,128)S(1)} %bitcast.85), channel_id=1, source_target_pairs={{0,4},{4,8},{8,12},{12,16},{16,20},{20,24},{24,28},{28,32},{32,36}... | collective-permute-start | bytes 442376 | tf_op jit(solution)/shard_map/ppermute | solution.py:24
  15.3 9.5 %collective-permute-start.1 = (f32[4,9,8,128]{3,2,1,0:T(8,128)S(1)}, f32[4,9,8,128]{3,2,1,0:T(8,128)S(1)}, u32[]{:S(2)}, u32[]{:S(2)}) collective-permute-start(f32[4,9,8,128]{3,2,1,0:T(8,128)S(1)} %bitcast.84), channel_id=1, source_target_pairs={{0,60},{4,0},{8,4},{12,8},{16,12},{20,16},{24,20},{28,24},{32,28},... | collective-permute-start | bytes 442376 | tf_op jit(solution)/shard_map/ppermute | solution.py:24
  25.5 1.4 collective-permute-done.1.south_ref
  27.8 4.1 %collective-permute-start.2 = (f32[9,8,128]{2,1,0:T(8,128)S(1)}, f32[9,8,128]{2,1,0:T(8,128)S(1)}, u32[]{:S(2)}, u32[]{:S(2)}) collective-permute-start(f32[9,8,128]{2,1,0:T(8,128)S(1)} %get-tuple-element.10), channel_id=1, source_target_pairs={{0,64},{64,128},{128,192},{192,256},{256,320},{320,384},{384,448},... | collective-permute-start | bytes 110600 | tf_op jit(solution)/shard_map/ppermute | solution.py:24
  32.9 2.3 %collective-permute-done.3.east_ref = f32[9,8,128]{2,1,0:T(8,128)S(1)} collective-permute-done((f32[9,8,128]{2,1,0:T(8,128)S(1)}, f32[9,8,128]{2,1,0:T(8,128)S(1)}, u32[]{:S(2)}, u32[]{:S(2)}) %collective-permute-start.3) | collective-permute-done | bytes 36896 | tf_op jit(solution)/shard_map/ppermute | solution.py:24
  35.2 5.6 %smooth.2 = f32[4,9,2,8,128]{4,3,2,1,0:T(8,128)} custom-call(s32[2]{0:T(128)S(1)} %pad_add_fusion.place_ref, f32[4,9,2,16,128]{4,3,2,1,0:T(8,128)S(1)} %get-tuple-element.9.full_ref, f32[9,8,128]{2,1,0:T(8,128)S(1)} %collective-permute-done.2.west_ref, f32[9,8,128]{2,1,0:T(8,128)S(1)} %collective-permute-done.3.east_ref), custom_call_target="tpu_custom_call" | custom-call | tf_op jit(solution)/shard_map/smooth/pallas_call | solution.py:132
  40.9 3.5 %all-to-all-start.1 = ((f32[4,9,2,8,128]{4,3,2,1,0:T(8,128)}), f32[4,9,2,8,128]{4,3,2,1,0:T(8,128)S(1)}, u32[]{:S(2)}, u32[]{:S(2)}) async-start(f32[4,9,2,8,128]{4,3,2,1,0:T(8,128)} %smooth.2), calls=%async_computation.1 | async-start | bytes 589824 | tf_op jit(solution)/shard_map/all_to_all | solution.py:141
  44.4 6.9 %all-to-all-done.1 = f32[4,9,2,8,128]{4,3,2,1,0:T(8,128)S(1)} async-done(((f32[4,9,2,8,128]{4,3,2,1,0:T(8,128)}), f32[4,9,2,8,128]{4,3,2,1,0:T(8,128)S(1)}, u32[]{:S(2)}, u32[]{:S(2)}) %all-to-all-start.1) | async-done | bytes 294944 | tf_op jit(solution)/shard_map/all_to_all | solution.py:141
  54.4 36.5 %all_to_all.42 = bf16[128,2,512]{2,1,0:T(2,128)(2,1)S(1)} all-to-all(bf16[128,2,512]{2,1,0:T(2,128)(2,1)S(1)} %broadcast_select_fusion.1), channel_id=1, replica_groups=mesh['lon_0'=4,'lon_1'=2,'lat'=16,'lev'=4] {'lon_0','lon_1','lat'}, dimensions={0} | all-to-all | bytes 524288 | tf_op jit(solution)/shard_map/all_to_all | solution.py:178
  94.0 5.7 %all-to-all-start.3 = ((bf16[128,2,512]{2,1,0:T(2,128)(2,1)}), bf16[128,2,512]{2,1,0:T(2,128)(2,1)S(1)}, u32[]{:S(2)}, u32[]{:S(2)}) async-start(bf16[128,2,512]{2,1,0:T(2,128)(2,1)} %bitcast.76), calls=%async_computation.3 | async-start | bytes 524288 | tf_op jit(solution)/shard_map/all_to_all | solution.py:186
  99.8 22.9 %all-to-all-done.3 = bf16[128,2,512]{2,1,0:T(2,128)(2,1)S(1)} async-done(((bf16[128,2,512]{2,1,0:T(2,128)(2,1)}), bf16[128,2,512]{2,1,0:T(2,128)(2,1)S(1)}, u32[]{:S(2)}, u32[]{:S(2)}) %all-to-all-start.3) | async-done | bytes 262176 | tf_op jit(solution)/shard_map/all_to_all | solution.py:186
  123.4 10.1 %all_to_all.43.own_ref = f32[4,9,2,8,128]{4,3,2,1,0:T(8,128)S(1)} all-to-all(f32[4,9,2,8,128]{4,3,2,1,0:T(8,128)S(1)} %bitcast.80), channel_id=1, replica_groups=mesh['lon_0'=4,'lon_1'=2,'lat'=16,'lev'=4] {'lev'}, dimensions={0} | all-to-all | bytes 589824 | tf_op jit(solution)/shard_map/all_to_all | solution.py:114
  133.5 2.1 %collective-permute-start.4 = (f32[4,9,8,128]{3,2,1,0:T(8,128)S(1)}, f32[4,9,8,128]{3,2,1,0:T(8,128)S(1)}, u32[]{:S(2)}, u32[]{:S(2)}) collective-permute-start(f32[4,9,8,128]{3,2,1,0:T(8,128)S(1)} %bitcast.87), channel_id=1, source_target_pairs={{0,4},{4,8},{8,12},{12,16},{16,20},{20,24},{24,28},{28,32},{32,36}... | collective-permute-start | bytes 442376 | tf_op jit(solution)/shard_map/ppermute | solution.py:24
  135.6 4.4 %collective-permute-start.5 = (f32[4,9,8,128]{3,2,1,0:T(8,128)S(1)}, f32[4,9,8,128]{3,2,1,0:T(8,128)S(1)}, u32[]{:S(2)}, u32[]{:S(2)}) collective-permute-start(f32[4,9,8,128]{3,2,1,0:T(8,128)S(1)} %bitcast.86), channel_id=1, source_target_pairs={{0,60},{4,0},{8,4},{12,8},{16,12},{20,16},{24,20},{28,24},{32,28},... | collective-permute-start | bytes 442376 | tf_op jit(solution)/shard_map/ppermute | solution.py:24
  140.0 1.6 collective-permute-done.4.north_ref
  143.4 1.7 collective-permute-start.6
  146.2 2.6 %collective-permute-done.7.east_ref = f32[9,8,128]{2,1,0:T(8,128)S(1)} collective-permute-done((f32[9,8,128]{2,1,0:T(8,128)S(1)}, f32[9,8,128]{2,1,0:T(8,128)S(1)}, u32[]{:S(2)}, u32[]{:S(2)}) %collective-permute-start.7) | collective-permute-done | bytes 36896 | tf_op jit(solution)/shard_map/ppermute | solution.py:24
  148.8 4.9 %smooth.3 = f32[4,9,2,8,128]{4,3,2,1,0:T(8,128)S(1)} custom-call(s32[2]{0:T(128)S(1)} %pad_add_fusion.place_ref, f32[4,9,2,16,128]{4,3,2,1,0:T(8,128)S(1)} %get-tuple-element.12.full_ref, f32[9,8,128]{2,1,0:T(8,128)S(1)} %collective-permute-done.6.west_ref, f32[9,8,128]{2,1,0:T(8,128)S(1)} %collective-permute-done.7.east_ref), custom_call_target="tpu_custom_call" | custom-call | tf_op jit(solution)/shard_map/smooth/pallas_call | solution.py:132
  153.8 8.3 %all_to_all.44 = f32[4,9,2,8,128]{4,3,2,1,0:T(8,128)S(1)} all-to-all(f32[4,9,2,8,128]{4,3,2,1,0:T(8,128)S(1)} %smooth.3), channel_id=1, replica_groups=mesh['lon_0'=4,'lon_1'=2,'lat'=16,'lev'=4] {'lev'}, dimensions={0} | all-to-all | bytes 589824 | tf_op jit(solution)/shard_map/all_to_all | solution.py:141
  162.9 2.7 %select_maximum_fusion = f32[128]{0:T(128)S(1)} fusion(f32[1]{0:T(128)} %bitcast.29, f32[1]{0:T(128)} %bitcast.28, f32[1]{0:T(128)} %bitcast.27, f32[1]{0:T(128)} %bitcast), kind=kLoop, calls=%fused_computation.44 | loop fusion | flops 1024 | bytes 528 | tf_op jit(solution)/shard_map/stack | solution.py:197
  165.6 20.7 %all_to_all.45 = f32[64,1,128]{2,1,0:T(1,128)S(1)} all-to-all(f32[64,1,128]{2,1,0:T(1,128)S(1)} %broadcast_in_dim.41), channel_id=1, replica_groups=mesh['lon_0'=4,'lon_1'=2,'lat'=16,'lev'=4] {'lat','lev'}, dimensions={0} | all-to-all | bytes 65536 | tf_op jit(solution)/shard_map/all_to_all | solution.py:30
  186.3 10.0 %all_to_all.46 = f32[8,1,128]{2,1,0:T(1,128)S(1)} all-to-all(f32[8,1,128]{2,1,0:T(1,128)S(1)} %broadcast_in_dim.42), channel_id=1, replica_groups=mesh['lon_0'=4,'lon_1'=2,'lat'=16,'lev'=4] {'lon_0','lon_1'}, dimensions={0} | all-to-all | bytes 8192 | tf_op jit(solution)/shard_map/all_to_all | solution.py:30
  (61 shorter events, 15.8 us)
Async XLA Ops:
  0.6 90.3 %copy-start = (bf16[1,1,1,128,2,8,512]{6,5,4,3,2,1,0:T(8,128)(2,1)S(1)}, bf16[1,1,1,128,2,8,512]{6,5,4,3,2,1,0:T(8,128)(2,1)}, u32[]{:S(2)}) copy-start(bf16[1,1,1,128,2,8,512]{6,5,4,3,2,1,0:T(8,128)(2,1)} %param.16) | copy-start | bytes 6291460
  0.6 43.7 %copy-start.7 = (s32[1,1,1,128]{3,2,1,0:T(1,128)S(1)}, s32[1,1,1,128]{3,2,1,0:T(1,128)}, u32[]{:S(2)}) copy-start(s32[1,1,1,128]{3,2,1,0:T(1,128)} %param.15) | copy-start | bytes 1540
  0.7 10.8 %all-to-all-start = ((f32[4,9,2,8,128]{4,3,2,1,0:T(8,128)}), f32[4,9,2,8,128]{4,3,2,1,0:T(8,128)S(1)}, u32[]{:S(2)}, u32[]{:S(2)}) async-start(f32[4,9,2,8,128]{4,3,2,1,0:T(8,128)} %bitcast.77), calls=%async_computation | async-start | bytes 589824 | tf_op jit(solution)/shard_map/all_to_all | solution.py:114
  6.6 45.9 %copy-start.5 = (f32[4,2,8,128]{3,2,1,0:T(8,128)S(1)}, f32[4,2,8,128]{3,2,1,0:T(8,128)}, u32[]{:S(2)}) copy-start(f32[4,2,8,128]{3,2,1,0:T(8,128)} %param.13) | copy-start | bytes 98308
  11.6 13.9 %collective-permute-start = (f32[4,9,8,128]{3,2,1,0:T(8,128)S(1)}, f32[4,9,8,128]{3,2,1,0:T(8,128)S(1)}, u32[]{:S(2)}, u32[]{:S(2)}) collective-permute-start(f32[4,9,8,128]{3,2,1,0:T(8,128)S(1)} %bitcast.85), channel_id=1, source_target_pairs={{0,4},{4,8},{8,12},{12,16},{16,20},{20,24},{24,28},{28,32},{32,36}... | collective-permute-start | bytes 442376 | tf_op jit(solution)/shard_map/ppermute | solution.py:24
  15.3 11.6 %collective-permute-start.1 = (f32[4,9,8,128]{3,2,1,0:T(8,128)S(1)}, f32[4,9,8,128]{3,2,1,0:T(8,128)S(1)}, u32[]{:S(2)}, u32[]{:S(2)}) collective-permute-start(f32[4,9,8,128]{3,2,1,0:T(8,128)S(1)} %bitcast.84), channel_id=1, source_target_pairs={{0,60},{4,0},{8,4},{12,8},{16,12},{20,16},{24,20},{28,24},{32,28},... | collective-permute-start | bytes 442376 | tf_op jit(solution)/shard_map/ppermute | solution.py:24
  27.8 5.1 %collective-permute-start.2 = (f32[9,8,128]{2,1,0:T(8,128)S(1)}, f32[9,8,128]{2,1,0:T(8,128)S(1)}, u32[]{:S(2)}, u32[]{:S(2)}) collective-permute-start(f32[9,8,128]{2,1,0:T(8,128)S(1)} %get-tuple-element.10), channel_id=1, source_target_pairs={{0,64},{64,128},{128,192},{192,256},{256,320},{320,384},{384,448},... | collective-permute-start | bytes 110600 | tf_op jit(solution)/shard_map/ppermute | solution.py:24
  31.8 3.4 %collective-permute-start.3 = (f32[9,8,128]{2,1,0:T(8,128)S(1)}, f32[9,8,128]{2,1,0:T(8,128)S(1)}, u32[]{:S(2)}, u32[]{:S(2)}) collective-permute-start(f32[9,8,128]{2,1,0:T(8,128)S(1)} %get-tuple-element.11), channel_id=1, source_target_pairs={{0,448},{64,0},{128,64},{192,128},{256,192},{320,256},{384,320},{4... | collective-permute-start | bytes 110600 | tf_op jit(solution)/shard_map/ppermute | solution.py:24
  40.9 10.4 %all-to-all-start.1 = ((f32[4,9,2,8,128]{4,3,2,1,0:T(8,128)}), f32[4,9,2,8,128]{4,3,2,1,0:T(8,128)S(1)}, u32[]{:S(2)}, u32[]{:S(2)}) async-start(f32[4,9,2,8,128]{4,3,2,1,0:T(8,128)} %smooth.2), calls=%async_computation.1 | async-start | bytes 589824 | tf_op jit(solution)/shard_map/all_to_all | solution.py:141
  91.0 1.1 copy-start.6
  92.2 31.0 %copy-start.2 = (bf16[32,4,2,8,128]{4,3,2,1,0:T(8,128)(2,1)S(1)}, bf16[32,4,2,8,128]{4,3,2,1,0:T(8,128)(2,1)}, u32[]{:S(2)}) copy-start(bf16[32,4,2,8,128]{4,3,2,1,0:T(8,128)(2,1)} %param.12) | copy-start | bytes 1572868
  94.0 28.8 %all-to-all-start.3 = ((bf16[128,2,512]{2,1,0:T(2,128)(2,1)}), bf16[128,2,512]{2,1,0:T(2,128)(2,1)S(1)}, u32[]{:S(2)}, u32[]{:S(2)}) async-start(bf16[128,2,512]{2,1,0:T(2,128)(2,1)} %bitcast.76), calls=%async_computation.3 | async-start | bytes 524288 | tf_op jit(solution)/shard_map/all_to_all | solution.py:186
  123.3 38.8 %copy-start.1 = (f32[36,2,8,128]{3,2,1,0:T(8,128)S(1)}, f32[36,2,8,128]{3,2,1,0:T(8,128)}, u32[]{:S(2)}) copy-start(f32[36,2,8,128]{3,2,1,0:T(8,128)} %param.11) | copy-start | bytes 884740
  123.4 38.8 %copy-start.3 = (f32[36,2,8,128]{3,2,1,0:T(8,128)S(1)}, f32[36,2,8,128]{3,2,1,0:T(8,128)}, u32[]{:S(2)}) copy-start(f32[36,2,8,128]{3,2,1,0:T(8,128)} %param.10) | copy-start | bytes 884740
  123.4 77.6 %copy-start.4 = (f32[36,2,8,128]{3,2,1,0:T(8,128)S(1)}, f32[36,2,8,128]{3,2,1,0:T(8,128)}, u32[]{:S(2)}) copy-start(f32[36,2,8,128]{3,2,1,0:T(8,128)} %param.9) | copy-start | bytes 884740
  133.5 8.1 %collective-permute-start.4 = (f32[4,9,8,128]{3,2,1,0:T(8,128)S(1)}, f32[4,9,8,128]{3,2,1,0:T(8,128)S(1)}, u32[]{:S(2)}, u32[]{:S(2)}) collective-permute-start(f32[4,9,8,128]{3,2,1,0:T(8,128)S(1)} %bitcast.87), channel_id=1, source_target_pairs={{0,4},{4,8},{8,12},{12,16},{16,20},{20,24},{24,28},{28,32},{32,36}... | collective-permute-start | bytes 442376 | tf_op jit(solution)/shard_map/ppermute | solution.py:24
  135.6 6.9 %collective-permute-start.5 = (f32[4,9,8,128]{3,2,1,0:T(8,128)S(1)}, f32[4,9,8,128]{3,2,1,0:T(8,128)S(1)}, u32[]{:S(2)}, u32[]{:S(2)}) collective-permute-start(f32[4,9,8,128]{3,2,1,0:T(8,128)S(1)} %bitcast.86), channel_id=1, source_target_pairs={{0,60},{4,0},{8,4},{12,8},{16,12},{20,16},{24,20},{28,24},{32,28},... | collective-permute-start | bytes 442376 | tf_op jit(solution)/shard_map/ppermute | solution.py:24
  143.4 2.8 %collective-permute-start.6 = (f32[9,8,128]{2,1,0:T(8,128)S(1)}, f32[9,8,128]{2,1,0:T(8,128)S(1)}, u32[]{:S(2)}, u32[]{:S(2)}) collective-permute-start(f32[9,8,128]{2,1,0:T(8,128)S(1)} %get-tuple-element.13), channel_id=1, source_target_pairs={{0,64},{64,128},{128,192},{192,256},{256,320},{320,384},{384,448},... | collective-permute-start | bytes 110600 | tf_op jit(solution)/shard_map/ppermute | solution.py:24
  145.2 3.7 %collective-permute-start.7 = (f32[9,8,128]{2,1,0:T(8,128)S(1)}, f32[9,8,128]{2,1,0:T(8,128)S(1)}, u32[]{:S(2)}, u32[]{:S(2)}) collective-permute-start(f32[9,8,128]{2,1,0:T(8,128)S(1)} %get-tuple-element.14), channel_id=1, source_target_pairs={{0,448},{64,0},{128,64},{192,128},{256,192},{320,256},{384,320},{4... | collective-permute-start | bytes 110600 | tf_op jit(solution)/shard_map/ppermute | solution.py:24

commit v2 on v1

v2 whole, which is shorter than its diff:
```python
import jax
import jax.numpy as jnp
from jax import lax
from jax.experimental import pallas as pl
from jax.experimental.pallas import tpu as pltpu
from jax.sharding import Mesh
from jax.sharding import PartitionSpec as P

LON = ("lon_0", "lon_1")
LON_LAT = ("lon_0", "lon_1", "lat")


spread_lon = 0.075
spread_lat = 0.3
spread_lev = 0.075
ens_share = 0.75
static_part = 0.5
HALO = 4
VMEM_BYTES = 12 * 1024 * 1024


def shift(x, axis, step):
    devices = lax.axis_size(axis)
    return lax.ppermute(x, axis, [(i, (i + step) % devices) for i in range(devices)])


def pack_kernel(own_ref, north_ref, south_ref, full_ref, first_ref, last_ref):
    groups, fields, planes = full_ref.shape[:3]
    row = lax.broadcasted_iota(jnp.int32, (8, 128), 0)

    def one_field(f, carry):
        rows = []
        for q in range(groups):
            north = north_ref[q, f]
            south = south_ref[q, f]
            for j in range(planes):
                own = pltpu.roll(own_ref[q, f, j], 4, 0)
                above = north if j == 0 else pltpu.roll(north, 4, 0)
                below = pltpu.roll(south, 4, 0) if j == 0 else south
                top = jnp.where(row < 4, above, own)
                bottom = jnp.where(row < 4, own, below)
                full_ref[q, f, j, 0:8] = top
                full_ref[q, f, j, 8:16] = bottom
                rows += [top, bottom]
        columns = jnp.concatenate(rows, axis=0).T
        first_ref[f] = columns[0:8]
        last_ref[f] = columns[120:128]
        return carry

    lax.fori_loop(0, fields, one_field, 0)


def inside_rows(place_ref, shape, axis):
    row = lax.broadcasted_iota(jnp.int32, shape, axis) % 16
    low = jnp.where(place_ref[0] == 0, HALO, 0)
    high = jnp.where(place_ref[0] == place_ref[1] - 1, 16 - HALO, 16)
    return jnp.where((row >= low) & (row < high), 1.0, 0.0).astype(jnp.float32)


centre_part = 1.0 - 2.0 * (spread_lon + spread_lat + spread_lev)


def strip_passes(place_ref, first_ref, last_ref, west_ref, east_ref, near_ref, far_ref):
    shape = first_ref.shape
    sub = lax.broadcasted_iota(jnp.int32, shape, 1)
    lane = lax.broadcasted_iota(jnp.int32, shape, 2)
    inside = inside_rows(place_ref, shape, 2)
    upper = sub >= 4
    left = pltpu.roll(jnp.where(upper, west_ref[...], first_ref[...]), 4, 1) * inside
    right = pltpu.roll(jnp.where(upper, last_ref[...], east_ref[...]), 4, 1) * inside

    def one_pass(x):
        beside = pltpu.roll(x, 1, 1) + pltpu.roll(x, 7, 1)
        across = pltpu.roll(x, 1, 2) + pltpu.roll(x, 127, 2)
        below = jnp.where(lane < 16, 0.0, pltpu.roll(x, 16, 2))
        above = jnp.where(lane >= 112, 0.0, pltpu.roll(x, 112, 2))
        result = centre_part * x + spread_lon * beside
        result = result + spread_lat * across
        result = result + spread_lev * (above + below)
        return result * inside

    near = jnp.zeros(shape, jnp.float32)
    for step in range(4):
        near = jnp.where(sub == 2 * step, pltpu.roll(left, (2 * step - 3) % 8, 1), near)
        if step == 0:
            far_ref[...] = jnp.where(sub == 7, pltpu.roll(right, 3, 1), 0.0)
        else:
            near = jnp.where(sub == 2 * step - 1, pltpu.roll(right, (2 * step - 5) % 8, 1), near)
        if step < 3:
            left, right = one_pass(left), one_pass(right)
    near_ref[...] = near


def field_passes(inside, x, near, far):
    total = x.shape[0]
    lane = lax.broadcasted_iota(jnp.int32, (total, 128), 1)
    left_edge = lane == 0
    right_edge = lane == 127
    blank = jnp.zeros((16, 128), jnp.float32)
    edges = jnp.concatenate([near, jnp.zeros((112, 128), jnp.float32), far], axis=0).T
    x = x * inside
    for step in range(4):
        edge = edges if step == 0 else pltpu.roll(edges, 128 - 2 * step, 1)
        beside = jnp.where(left_edge, edge, pltpu.roll(x, 1, 1)) + jnp.where(
            right_edge, edge, pltpu.roll(x, 127, 1)
        )
        across = pltpu.roll(x, 1, 0) + pltpu.roll(x, total - 1, 0)
        above = jnp.concatenate([x[16:], blank], axis=0)
        below = jnp.concatenate([blank, x[: total - 16]], axis=0)
        result = centre_part * x + spread_lon * beside
        result = result + spread_lat * across
        result = result + spread_lev * (above + below)
        x = result * inside
    return x


def middle_rows(x, plane):
    sub = lax.broadcasted_iota(jnp.int32, (8, 128), 0)
    top = pltpu.roll(x[plane * 16 : plane * 16 + 8], 4, 0)
    bottom = pltpu.roll(x[plane * 16 + 8 : plane * 16 + 16], 4, 0)
    return jnp.where(sub < 4, top, bottom)


def smooth_kernel(
    place_ref, full_ref, first_ref, last_ref, west_ref, east_ref, out_ref, near_ref, far_ref
):
    groups, fields, planes = full_ref.shape[:3]
    total = groups * planes * 16
    strip_passes(place_ref, first_ref, last_ref, west_ref, east_ref, near_ref, far_ref)
    inside = inside_rows(place_ref, (total, 128), 0)

    def one_field(f, carry):
        x = full_ref[:, f].reshape(total, 128)
        x = field_passes(inside, x, near_ref[f], far_ref[f])
        for q in range(groups):
            for j in range(planes):
                out_ref[q, f, j] = middle_rows(x, q * planes + j)
        return carry

    lax.fori_loop(0, fields, one_field, 0)


def image_kernel(
    place_ref,
    full_ref,
    first_ref,
    last_ref,
    west_ref,
    east_ref,
    pair_ref,
    out_ref,
    near_ref,
    far_ref,
):
    groups, fields, planes = full_ref.shape[:3]
    total = groups * planes * 16
    strip_passes(place_ref, first_ref, last_ref, west_ref, east_ref, near_ref, far_ref)
    inside = inside_rows(place_ref, (total, 128), 0)

    def one_field(f, sums):
        x = full_ref[:, f].reshape(total, 128)
        x = field_passes(inside, x, near_ref[f], far_ref[f])
        start_norm, curvature, crossed, squared = sums
        for q in range(groups):
            for j in range(planes):
                direction = pair_ref[q, f, j]
                residual = pair_ref[q, fields + f, j]
                image = direction + middle_rows(x, q * planes + j)
                out_ref[q, f, j] = image
                start_norm = start_norm + residual * residual
                curvature = curvature + direction * image
                crossed = crossed + residual * image
                squared = squared + image * image
        return (start_norm, curvature, crossed, squared)

    zero = jnp.zeros((8, 128), jnp.float32)
    sums = lax.fori_loop(0, fields, one_field, (zero, zero, zero, zero))
    lane = lax.broadcasted_iota(jnp.int32, (8, 128), 1)
    row = zero
    for k in range(4):
        part = jnp.broadcast_to(jnp.sum(sums[k], axis=0, keepdims=True), (8, 128))
        part = part + pltpu.roll(part, 64, 1)
        part = part + pltpu.roll(part, 32, 1)
        row = jnp.where((lane >= 32 * k) & (lane < 32 * k + 32), part, row)
    for q in range(groups):
        out_ref[q, fields, 0] = row
        out_ref[q, fields, 1] = row


def update_kernel(
    rows_ref,
    image_ref,
    solution_ref,
    residual_ref,
    direction_ref,
    new_solution_ref,
    new_residual_ref,
    new_direction_ref,
):
    groups, fields, planes = solution_ref.shape[:3]
    row = jnp.sum(rows_ref[...], axis=0, keepdims=True)
    lane = lax.broadcasted_iota(jnp.int32, (1, 128), 1)
    start_norm, curvature, crossed, squared = (
        jnp.sum(
            jnp.where((lane >= 32 * k) & (lane < 32 * k + 32), row, 0.0), axis=1, keepdims=True
        )
        for k in range(4)
    )
    step_size = start_norm / curvature
    next_norm = start_norm - 2.0 * step_size * crossed + step_size * step_size * squared
    ratio = next_norm / (start_norm + 1e-06)
    step_size = jnp.broadcast_to(step_size, (8, 128))
    ratio = jnp.broadcast_to(ratio, (8, 128))

    def one_field(f, carry):
        for q in range(groups):
            for j in range(planes):
                direction = direction_ref[q, f, j]
                new_residual = residual_ref[q, f, j] - step_size * image_ref[q, f, j]
                new_solution_ref[q, f, j] = solution_ref[q, f, j] + step_size * direction
                new_residual_ref[q, f, j] = new_residual
                new_direction_ref[q, f, j] = new_residual + ratio * direction
        return carry

    lax.fori_loop(0, fields, one_field, 0)


def swap_lev(blocks):
    return lax.all_to_all(blocks, "lev", split_axis=0, concat_axis=0, tiled=True)


def local_call(kernel, out_shape, scalars, name, scratch=()):
    def run(*operands):
        in_specs = [pl.BlockSpec(memory_space=pltpu.SMEM)] * scalars
        in_specs += [pl.BlockSpec(memory_space=pltpu.VMEM)] * (len(operands) - scalars)
        return pl.pallas_call(
            kernel,
            out_shape=out_shape,
            in_specs=in_specs,
            out_specs=jax.tree.map(lambda _: pl.BlockSpec(memory_space=pltpu.VMEM), out_shape),
            scratch_shapes=list(scratch),
            compiler_params=pltpu.CompilerParams(vmem_limit_bytes=VMEM_BYTES),
            name=name,
        )(*operands)

    return run


def smooth(blocks, share, tail=None):
    groups, _, levels, lat_rows, lon_cells = blocks.shape
    own = blocks[:, :share]
    halo_shape = (groups, share, levels * HALO, lon_cells)
    north = shift(own[..., lat_rows - HALO :, :].reshape(halo_shape), "lat", 1)
    south = shift(own[..., :HALO, :].reshape(halo_shape), "lat", -1)
    strip = jax.ShapeDtypeStruct((share, 8, 128), jnp.float32)
    full = jax.ShapeDtypeStruct((groups, share, levels, 16, lon_cells), jnp.float32)
    full, first, last = local_call(pack_kernel, (full, strip, strip), 0, "pack")(
        blocks, north, south
    )
    west = shift(last, LON, 1)
    east = shift(first, LON, -1)
    place = jnp.stack([lax.axis_index("lat"), lax.axis_size("lat")]).astype(jnp.int32)
    scratch = [pltpu.VMEM((share, 8, 128), jnp.float32)] * 2
    operands = (place, full, first, last, west, east)
    shape = [groups, share, levels, lat_rows, lon_cells]
    if tail is None:
        out = jax.ShapeDtypeStruct(tuple(shape), jnp.float32)
        return local_call(smooth_kernel, out, 1, "smooth", scratch)(*operands)
    shape[1] += 1
    out = jax.ShapeDtypeStruct(tuple(shape), jnp.float32)
    return local_call(image_kernel, out, 1, "image", scratch)(*operands, tail)


def body(
    solution,
    residual,
    direction,
    ensemble,
    static_sd,
    send_tile,
    pair_count,
    obs_weight,
    obs_precision,
):
    members, variables, levels, lat_rows, lon_cells = ensemble.shape
    scale_ens = (ens_share / members) ** 0.5
    tile_width = variables * lon_cells
    tile_total = levels * lat_rows
    group_size = send_tile.shape[3]
    slot_count = send_tile.shape[4]
    obs_count = obs_weight.shape[5]
    groups = lax.axis_size("lev")
    share = direction.shape[0] // groups
    grouped = (groups, share, levels, lat_rows, lon_cells)
    pair = swap_lev(
        jnp.concatenate([direction.reshape(grouped), residual.reshape(grouped)], axis=1)
    )
    smoothed = swap_lev(smooth(pair, share)).reshape(direction.shape)
    ens_part = jnp.sum(ensemble * smoothed[:members, None], axis=0)
    increment = (scale_ens * ens_part + static_part * static_sd * smoothed[members:]).astype(
        jnp.bfloat16
    )
    tile_table = increment.transpose(1, 2, 0, 3).reshape(tile_total, tile_width)
    tile_pick = send_tile.reshape(group_size * slot_count)
    is_live = (
        jnp.arange(slot_count, dtype=jnp.int32)[None, :] < pair_count.reshape(group_size)[:, None]
    )
    outgoing = jnp.take(tile_table, tile_pick, axis=0)
    outgoing = jnp.where(
        is_live.reshape(group_size * slot_count)[:, None], outgoing, jnp.zeros_like(outgoing)
    )
    outgoing = outgoing.reshape(group_size, slot_count, tile_width)
    arrived = lax.all_to_all(outgoing, LON_LAT, split_axis=0, concat_axis=0, tiled=True)
    weights = obs_weight.reshape(group_size, slot_count, obs_count, tile_width)
    predicted = jnp.einsum("gsbc,gsc->gsb", weights, arrived, preferred_element_type=jnp.float32)
    weighted = (obs_precision.reshape(group_size, slot_count, obs_count) * predicted).astype(
        jnp.bfloat16
    )
    returned = jnp.einsum("gsbc,gsb->gsc", weights, weighted, preferred_element_type=jnp.float32)
    returned = returned.astype(jnp.bfloat16)
    came_back = lax.all_to_all(returned, LON_LAT, split_axis=0, concat_axis=0, tiled=True)
    came_back = came_back.reshape(group_size * slot_count, tile_width)
    one_hot = (tile_pick[:, None] == jnp.arange(tile_total, dtype=jnp.int32)[None, :]).astype(
        jnp.bfloat16
    )
    adj_tiles = jnp.dot(one_hot.T, came_back, preferred_element_type=jnp.float32)
    adjoint = adj_tiles.reshape(levels, lat_rows, variables, lon_cells).transpose(2, 0, 1, 3)
    back_ens = scale_ens * jnp.sum(ensemble * adjoint[None], axis=1)
    back_static = static_part * static_sd * adjoint
    back = jnp.concatenate([back_ens, back_static], axis=0)
    image = swap_lev(smooth(swap_lev(back.reshape(grouped)), share, pair))
    peers = lax.axis_size(LON_LAT)
    row = jnp.sum(image[:, share, 0, 0, :], axis=0)
    rows = lax.all_to_all(
        jnp.broadcast_to(row, (peers, 1, lon_cells)), LON_LAT, split_axis=0, concat_axis=0, tiled=True
    )
    out = jax.ShapeDtypeStruct(grouped, jnp.float32)
    outs = local_call(update_kernel, (out, out, out), 0, "update")(
        rows.reshape(peers, lon_cells),
        image,
        solution.reshape(grouped),
        residual.reshape(grouped),
        direction.reshape(grouped),
    )
    return tuple(x.reshape(direction.shape) for x in outs)


def solution(mesh):
    split = Mesh(
        mesh.devices.reshape(4, 2, mesh.shape["lat"], mesh.shape["lev"]),
        ("lon_0", "lon_1", "lat", "lev"),
    )
    in_specs = (
        P(None, "lev", "lat", LON),
        P(None, "lev", "lat", LON),
        P(None, "lev", "lat", LON),
        P(None, None, "lev", "lat", LON),
        P(None, "lev", "lat", LON),
        P("lev", LON, "lat", None, None),
        P("lev", LON, "lat", None),
        P("lev", LON, "lat", None, None, None, None),
        P("lev", LON, "lat", None, None, None),
    )
    out_specs = (P(None, "lev", "lat", LON), P(None, "lev", "lat", LON), P(None, "lev", "lat", LON))
    return jax.shard_map(body, mesh=split, in_specs=in_specs, out_specs=out_specs, check_vma=False)
```

time: 203 us -> 196 us (0.966)
  between operations: 5.03 us -> 0.93 us
  waiting for transfers between devices: 45.3 us -> 41.3 us
  local copies, waits for them, and re-layouts: 4.7 us -> 7.31 us
    ppermute x8, waiting for transfers between devices: 10.7 us -> 6.38 us  [shift(): lax.ppermute(x, axis, [(i, (i + step) % devices) for i in range(devices)])]
    all_to_all x4 -> x3, blocking collectives: 49 us -> 45 us  [the longest x1 26.7 us: body(): lax.all_to_all(jnp.broadcast_to(row, (peers, 1, lon_cells)), LON_LAT, spl...]
    another operation x1 -> x0, other arithmetic: 2.7 us -> none  [body(): jnp.stack([jnp.sum(residual * residual), jnp.sum(direction * image_field)...]
    all_to_all x1, blocking collectives: 36.5 us -> 38.8 us  [body(): lax.all_to_all(outgoing, LON_LAT, split_axis=0, concat_axis=0, tiled=True)]
    concatenate x0 -> x1, other arithmetic: none -> 2.08 us  [body(): jnp.concatenate([direction.reshape(grouped), residual.reshape(grouped)],...]
    pallas_call x4 -> x5, Pallas kernels: 12.3 us -> 12.8 us  [run(): pl.pallas_call(kernel, out_shape=out_shape, in_specs=in_specs, out_specs=...]
  transfers between devices with their start and end apart: 11 -> 11, of which waited for: 10 -> 8; matrix products, arithmetic and copies ran while one was open for 1% -> 1% of each run, Pallas kernels for 0% -> 0%
where the time goes in v2:
time: 196 us
  blocking collectives  83.8 us (43%)
  starting transfers between devices  41.3 us (21%)
  waiting for transfers between devices  41.3 us (21%)
  Pallas kernels  12.8 us (7%)
  local copies, waits for them, and re-layouts  7.31 us (4%)
  other arithmetic  5.53 us (3%)
  matrix products  2.66 us (1%)
    all_to_all x1, blocking collectives, body(): lax.all_to_all(outgoing, LON_LAT, split_axis=0, concat_axis=0, tiled=True)  38.8 us
    ppermute x8, starting transfers between devices, shift(): lax.ppermute(x, axis, [(i, (i + step) % devices) for i in range(devices)])  27.1 us
    all_to_all x1, blocking collectives, body(): lax.all_to_all(jnp.broadcast_to(row, (peers, 1, lon_cells)), LON_LAT, spl...  26.7 us
    all_to_all x1, waiting for transfers between devices, body(): lax.all_to_all(returned, LON_LAT, split_axis=0, concat_axis=0, tiled=True)  22.9 us
    all_to_all x2, blocking collectives, swap_lev(): lax.all_to_all(blocks, 'lev', split_axis=0, concat_axis=0, tiled=True)  18.3 us
    pallas_call x5, Pallas kernels, run(): pl.pallas_call(kernel, out_shape=out_shape, in_specs=in_specs, out_specs=...  12.8 us
    all_to_all x2, waiting for transfers between devices, swap_lev(): lax.all_to_all(blocks, 'lev', split_axis=0, concat_axis=0, tiled=True)  11.9 us
    all_to_all x2, starting transfers between devices, swap_lev(): lax.all_to_all(blocks, 'lev', split_axis=0, concat_axis=0, tiled=True)  8.45 us
  transfers between devices with their start and end apart: 11, of which 8 were waited for; matrix products, arithmetic and copies ran while one was open for 1% of the time, Pallas kernels for 0%

profile of v2, /device:TPU:1, one launch (start us, length us, event | category | flops | bytes accessed | tf_op | source)
XLA Modules:
  0.0 195.6 jit_solution(995344481869520623)
XLA Ops:
  0.7 2.1 %pad_maximum_fusion = f32[4,18,2,8,128]{4,3,2,1,0:T(8,128)} fusion(f32[4,9,2,8,128]{4,3,2,1,0:T(8,128)} %bitcast.62, f32[4,9,2,8,128]{4,3,2,1,0:T(8,128)} %bitcast.64), kind=kLoop, calls=%fused_computation.10 | loop fusion | flops 147456 | bytes 1179648 | tf_op jit(solution)/shard_map/concatenate | solution.py:296
  2.7 5.0 %all-to-all-start = ((f32[4,18,2,8,128]{4,3,2,1,0:T(8,128)}), f32[4,18,2,8,128]{4,3,2,1,0:T(8,128)S(1)}, u32[]{:S(2)}, u32[]{:S(2)}) async-start(f32[4,18,2,8,128]{4,3,2,1,0:T(8,128)} %pad_maximum_fusion), calls=%async_computation | async-start | bytes 1179648 | tf_op jit(solution)/shard_map/all_to_all | solution.py:229
  8.0 7.0 %all-to-all-done.own_ref.pair_ref = f32[4,18,2,8,128]{4,3,2,1,0:T(8,128)S(1)} async-done(((f32[4,18,2,8,128]{4,3,2,1,0:T(8,128)}), f32[4,18,2,8,128]{4,3,2,1,0:T(8,128)S(1)}, u32[]{:S(2)}, u32[]{:S(2)}) %all-to-all-start) | async-done | bytes 589856 | tf_op jit(solution)/shard_map/all_to_all | solution.py:229
  15.1 5.6 %collective-permute-start = (f32[4,9,8,128]{3,2,1,0:T(8,128)S(1)}, f32[4,9,8,128]{3,2,1,0:T(8,128)S(1)}, u32[]{:S(2)}, u32[]{:S(2)}) collective-permute-start(f32[4,9,8,128]{3,2,1,0:T(8,128)S(1)} %bitcast.75), channel_id=1, source_target_pairs={{0,4},{4,8},{8,12},{12,16},{16,20},{20,24},{24,28},{28,32},{32,36}... | collective-permute-start | bytes 442376 | tf_op jit(solution)/shard_map/ppermute | solution.py:24
  20.7 9.5 %collective-permute-start.1 = (f32[4,9,8,128]{3,2,1,0:T(8,128)S(1)}, f32[4,9,8,128]{3,2,1,0:T(8,128)S(1)}, u32[]{:S(2)}, u32[]{:S(2)}) collective-permute-start(f32[4,9,8,128]{3,2,1,0:T(8,128)S(1)} %bitcast.74), channel_id=1, source_target_pairs={{0,60},{4,0},{8,4},{12,8},{16,12},{20,16},{24,20},{28,24},{32,28},... | collective-permute-start | bytes 442376 | tf_op jit(solution)/shard_map/ppermute | solution.py:24
  30.8 1.5 collective-permute-done.1.south_ref
  34.7 2.7 %collective-permute-start.3 = (f32[9,8,128]{2,1,0:T(8,128)S(1)}, f32[9,8,128]{2,1,0:T(8,128)S(1)}, u32[]{:S(2)}, u32[]{:S(2)}) collective-permute-start(f32[9,8,128]{2,1,0:T(8,128)S(1)} %get-tuple-element.13.first_ref), channel_id=1, source_target_pairs={{0,448},{64,0},{128,64},{192,128},{256,192},{320,256},{384,320},{4... | collective-permute-start | bytes 110600 | tf_op jit(solution)/shard_map/ppermute | solution.py:24
  40.2 5.3 %smooth.1 = f32[4,9,2,8,128]{4,3,2,1,0:T(8,128)} custom-call(s32[2]{0:T(128)S(1)} %pad_add_fusion.place_ref, f32[4,9,2,16,128]{4,3,2,1,0:T(8,128)S(1)} %get-tuple-element.12.full_ref, f32[9,8,128]{2,1,0:T(8,128)S(1)} %get-tuple-element.13.first_ref, f32[9,8,128]{2,1,0:T(8,128)S(1)} %get-tuple-element.14.last_ref, ...), custom_call_target="tpu_custom_call" | custom-call | tf_op jit(solution)/shard_map/smooth/pallas_call | solution.py:236
  45.5 3.5 %all-to-all-start.1 = ((f32[4,9,2,8,128]{4,3,2,1,0:T(8,128)}), f32[4,9,2,8,128]{4,3,2,1,0:T(8,128)S(1)}, u32[]{:S(2)}, u32[]{:S(2)}) async-start(f32[4,9,2,8,128]{4,3,2,1,0:T(8,128)} %smooth.1), calls=%async_computation.1 | async-start | bytes 589824 | tf_op jit(solution)/shard_map/all_to_all | solution.py:229
  49.7 4.9 %all-to-all-done.1 = f32[4,9,2,8,128]{4,3,2,1,0:T(8,128)S(1)} async-done(((f32[4,9,2,8,128]{4,3,2,1,0:T(8,128)}), f32[4,9,2,8,128]{4,3,2,1,0:T(8,128)S(1)}, u32[]{:S(2)}, u32[]{:S(2)}) %all-to-all-start.1) | async-done | bytes 294944 | tf_op jit(solution)/shard_map/all_to_all | solution.py:229
  54.6 1.2 fusion.4
  55.8 1.2 gather_fusion
  57.8 38.8 %all_to_all.35 = bf16[128,2,512]{2,1,0:T(2,128)(2,1)S(1)} all-to-all(bf16[128,2,512]{2,1,0:T(2,128)(2,1)S(1)} %broadcast_select_fusion.1), channel_id=1, replica_groups=mesh['lon_0'=4,'lon_1'=2,'lat'=16,'lev'=4] {'lon_0','lon_1','lat'}, dimensions={0} | all-to-all | bytes 524288 | tf_op jit(solution)/shard_map/all_to_all | solution.py:313
  99.6 5.7 %all-to-all-start.3 = ((bf16[128,2,512]{2,1,0:T(2,128)(2,1)}), bf16[128,2,512]{2,1,0:T(2,128)(2,1)S(1)}, u32[]{:S(2)}, u32[]{:S(2)}) async-start(bf16[128,2,512]{2,1,0:T(2,128)(2,1)} %bitcast.61), calls=%async_computation.3 | async-start | bytes 524288 | tf_op jit(solution)/shard_map/all_to_all | solution.py:321
  105.5 22.9 %all-to-all-done.3 = bf16[128,2,512]{2,1,0:T(2,128)(2,1)S(1)} async-done(((bf16[128,2,512]{2,1,0:T(2,128)(2,1)}), bf16[128,2,512]{2,1,0:T(2,128)(2,1)S(1)}, u32[]{:S(2)}, u32[]{:S(2)}) %all-to-all-start.3) | async-done | bytes 262176 | tf_op jit(solution)/shard_map/all_to_all | solution.py:321
  131.4 10.1 %all_to_all.36.own_ref = f32[4,9,2,8,128]{4,3,2,1,0:T(8,128)S(1)} all-to-all(f32[4,9,2,8,128]{4,3,2,1,0:T(8,128)S(1)} %bitcast.70), channel_id=1, replica_groups=mesh['lon_0'=4,'lon_1'=2,'lat'=16,'lev'=4] {'lev'}, dimensions={0} | all-to-all | bytes 589824 | tf_op jit(solution)/shard_map/all_to_all | solution.py:229
  141.5 2.1 %collective-permute-start.4 = (f32[4,9,8,128]{3,2,1,0:T(8,128)S(1)}, f32[4,9,8,128]{3,2,1,0:T(8,128)S(1)}, u32[]{:S(2)}, u32[]{:S(2)}) collective-permute-start(f32[4,9,8,128]{3,2,1,0:T(8,128)S(1)} %bitcast.77), channel_id=1, source_target_pairs={{0,4},{4,8},{8,12},{12,16},{16,20},{20,24},{24,28},{28,32},{32,36}... | collective-permute-start | bytes 442376 | tf_op jit(solution)/shard_map/ppermute | solution.py:24
  143.6 4.4 %collective-permute-start.5 = (f32[4,9,8,128]{3,2,1,0:T(8,128)S(1)}, f32[4,9,8,128]{3,2,1,0:T(8,128)S(1)}, u32[]{:S(2)}, u32[]{:S(2)}) collective-permute-start(f32[4,9,8,128]{3,2,1,0:T(8,128)S(1)} %bitcast.76), channel_id=1, source_target_pairs={{0,60},{4,0},{8,4},{12,8},{16,12},{20,16},{24,20},{28,24},{32,28},... | collective-permute-start | bytes 442376 | tf_op jit(solution)/shard_map/ppermute | solution.py:24
  148.1 1.6 collective-permute-done.4.north_ref
  151.4 1.7 collective-permute-start.7
  153.2 1.6 collective-permute-done.7.east_ref
  154.9 4.6 %image.1 = f32[4,10,2,8,128]{4,3,2,1,0:T(8,128)S(1)} custom-call(s32[2]{0:T(128)S(1)} %pad_add_fusion.place_ref, f32[4,9,2,16,128]{4,3,2,1,0:T(8,128)S(1)} %get-tuple-element.15.full_ref, f32[9,8,128]{2,1,0:T(8,128)S(1)} %get-tuple-element.16.first_ref, f32[9,8,128]{2,1,0:T(8,128)S(1)} %get-tuple-element.17.last_ref, ...), custom_call_target="tpu_custom_call" | custom-call | tf_op jit(solution)/shard_map/image/pallas_call | solution.py:236
  159.4 8.2 %all_to_all.37.image_ref = f32[4,10,2,8,128]{4,3,2,1,0:T(8,128)S(1)} all-to-all(f32[4,10,2,8,128]{4,3,2,1,0:T(8,128)S(1)} %image.1), channel_id=1, replica_groups=mesh['lon_0'=4,'lon_1'=2,'lat'=16,'lev'=4] {'lev'}, dimensions={0} | all-to-all | bytes 655360 | tf_op jit(solution)/shard_map/all_to_all | solution.py:229
  167.8 26.7 %all_to_all.38 = f32[128,1,128]{2,1,0:T(1,128)S(1)} all-to-all(f32[128,1,128]{2,1,0:T(1,128)S(1)} %broadcast_in_dim.32), channel_id=1, replica_groups=mesh['lon_0'=4,'lon_1'=2,'lat'=16,'lev'=4] {'lon_0','lon_1','lat'}, dimensions={0} | all-to-all | bytes 131072 | tf_op jit(solution)/shard_map/all_to_all | solution.py:334
  (64 shorter events, 16.9 us)
Async XLA Ops:
  0.6 95.9 %copy-start = (bf16[1,1,1,128,2,8,512]{6,5,4,3,2,1,0:T(8,128)(2,1)S(1)}, bf16[1,1,1,128,2,8,512]{6,5,4,3,2,1,0:T(8,128)(2,1)}, u32[]{:S(2)}) copy-start(bf16[1,1,1,128,2,8,512]{6,5,4,3,2,1,0:T(8,128)(2,1)} %param.16) | copy-start | bytes 6291460
  0.6 7.1 %copy-start.11 = (s32[1,1,1,128,2]{3,4,2,1,0:T(2,128)S(1)}, s32[1,1,1,128,2]{3,4,2,1,0:T(2,128)}, u32[]{:S(2)}) copy-start(s32[1,1,1,128,2]{3,4,2,1,0:T(2,128)} %param.14) | copy-start | bytes 3076
  2.7 12.3 %all-to-all-start = ((f32[4,18,2,8,128]{4,3,2,1,0:T(8,128)}), f32[4,18,2,8,128]{4,3,2,1,0:T(8,128)S(1)}, u32[]{:S(2)}, u32[]{:S(2)}) async-start(f32[4,18,2,8,128]{4,3,2,1,0:T(8,128)} %pad_maximum_fusion), calls=%async_computation | async-start | bytes 1179648 | tf_op jit(solution)/shard_map/all_to_all | solution.py:229
  7.9 7.2 %copy-start.7 = (s32[1,1,1,128,2]{4,3,2,1,0:T(8,128)}, s32[1,1,1,128,2]{4,3,2,1,0:T(8,128)S(1)}, u32[]{:S(2)}) copy-start(s32[1,1,1,128,2]{4,3,2,1,0:T(8,128)S(1)} %copy.25) | copy-start | bytes 3076
  15.0 40.8 %copy-start.9 = (f32[4,2,8,128]{3,2,1,0:T(8,128)S(1)}, f32[4,2,8,128]{3,2,1,0:T(8,128)}, u32[]{:S(2)}) copy-start(f32[4,2,8,128]{3,2,1,0:T(8,128)} %param.13) | copy-start | bytes 98308
  15.1 15.7 %collective-permute-start = (f32[4,9,8,128]{3,2,1,0:T(8,128)S(1)}, f32[4,9,8,128]{3,2,1,0:T(8,128)S(1)}, u32[]{:S(2)}, u32[]{:S(2)}) collective-permute-start(f32[4,9,8,128]{3,2,1,0:T(8,128)S(1)} %bitcast.75), channel_id=1, source_target_pairs={{0,4},{4,8},{8,12},{12,16},{16,20},{20,24},{24,28},{28,32},{32,36}... | collective-permute-start | bytes 442376 | tf_op jit(solution)/shard_map/ppermute | solution.py:24
  20.7 11.6 %collective-permute-start.1 = (f32[4,9,8,128]{3,2,1,0:T(8,128)S(1)}, f32[4,9,8,128]{3,2,1,0:T(8,128)S(1)}, u32[]{:S(2)}, u32[]{:S(2)}) collective-permute-start(f32[4,9,8,128]{3,2,1,0:T(8,128)S(1)} %bitcast.74), channel_id=1, source_target_pairs={{0,60},{4,0},{8,4},{12,8},{16,12},{20,16},{24,20},{28,24},{32,28},... | collective-permute-start | bytes 442376 | tf_op jit(solution)/shard_map/ppermute | solution.py:24
  32.3 0.7 copy-start.4
  32.9 0.9 copy-start.5
  34.7 5.4 %collective-permute-start.3 = (f32[9,8,128]{2,1,0:T(8,128)S(1)}, f32[9,8,128]{2,1,0:T(8,128)S(1)}, u32[]{:S(2)}, u32[]{:S(2)}) collective-permute-start(f32[9,8,128]{2,1,0:T(8,128)S(1)} %get-tuple-element.13.first_ref), channel_id=1, source_target_pairs={{0,448},{64,0},{128,64},{192,128},{256,192},{320,256},{384,320},{4... | collective-permute-start | bytes 110600 | tf_op jit(solution)/shard_map/ppermute | solution.py:24
  37.4 2.7 %collective-permute-start.2 = (f32[9,8,128]{2,1,0:T(8,128)S(1)}, f32[9,8,128]{2,1,0:T(8,128)S(1)}, u32[]{:S(2)}, u32[]{:S(2)}) collective-permute-start(f32[9,8,128]{2,1,0:T(8,128)S(1)} %get-tuple-element.14.last_ref), channel_id=1, source_target_pairs={{0,64},{64,128},{128,192},{192,256},{256,320},{320,384},{384,448},... | collective-permute-start | bytes 110600 | tf_op jit(solution)/shard_map/ppermute | solution.py:24
  45.5 9.1 %all-to-all-start.1 = ((f32[4,9,2,8,128]{4,3,2,1,0:T(8,128)}), f32[4,9,2,8,128]{4,3,2,1,0:T(8,128)S(1)}, u32[]{:S(2)}, u32[]{:S(2)}) async-start(f32[4,9,2,8,128]{4,3,2,1,0:T(8,128)} %smooth.1), calls=%async_computation.1 | async-start | bytes 589824 | tf_op jit(solution)/shard_map/all_to_all | solution.py:229
  96.6 1.1 copy-start.10
  97.6 7.7 %copy-start.8 = (s32[1,1,1,128,2]{4,3,2,1,0:T(8,128)S(1)}, s32[1,1,1,128,2]{4,3,2,1,0:T(8,128)}, u32[]{:S(2)}) copy-start(s32[1,1,1,128,2]{4,3,2,1,0:T(8,128)} %copy-done.7) | copy-start | bytes 3076
  97.8 33.4 %copy-start.6 = (bf16[32,4,2,8,128]{4,3,2,1,0:T(8,128)(2,1)S(1)}, bf16[32,4,2,8,128]{4,3,2,1,0:T(8,128)(2,1)}, u32[]{:S(2)}) copy-start(bf16[32,4,2,8,128]{4,3,2,1,0:T(8,128)(2,1)} %param.12) | copy-start | bytes 1572868
  99.6 28.8 %all-to-all-start.3 = ((bf16[128,2,512]{2,1,0:T(2,128)(2,1)}), bf16[128,2,512]{2,1,0:T(2,128)(2,1)S(1)}, u32[]{:S(2)}, u32[]{:S(2)}) async-start(bf16[128,2,512]{2,1,0:T(2,128)(2,1)} %bitcast.61), calls=%async_computation.3 | async-start | bytes 524288 | tf_op jit(solution)/shard_map/all_to_all | solution.py:321
  131.4 63.1 %copy-start.1 = (f32[36,2,8,128]{3,2,1,0:T(8,128)S(1)}, f32[36,2,8,128]{3,2,1,0:T(8,128)}, u32[]{:S(2)}) copy-start(f32[36,2,8,128]{3,2,1,0:T(8,128)} %param.10) | copy-start | bytes 884740
  131.4 63.1 %copy-start.2 = (f32[36,2,8,128]{3,2,1,0:T(8,128)S(1)}, f32[36,2,8,128]{3,2,1,0:T(8,128)}, u32[]{:S(2)}) copy-start(f32[36,2,8,128]{3,2,1,0:T(8,128)} %param.11) | copy-start | bytes 884740
  131.4 63.1 %copy-start.3 = (f32[36,2,8,128]{3,2,1,0:T(8,128)S(1)}, f32[36,2,8,128]{3,2,1,0:T(8,128)}, u32[]{:S(2)}) copy-start(f32[36,2,8,128]{3,2,1,0:T(8,128)} %param.9) | copy-start | bytes 884740
  141.5 8.1 %collective-permute-start.4 = (f32[4,9,8,128]{3,2,1,0:T(8,128)S(1)}, f32[4,9,8,128]{3,2,1,0:T(8,128)S(1)}, u32[]{:S(2)}, u32[]{:S(2)}) collective-permute-start(f32[4,9,8,128]{3,2,1,0:T(8,128)S(1)} %bitcast.77), channel_id=1, source_target_pairs={{0,4},{4,8},{8,12},{12,16},{16,20},{20,24},{24,28},{28,32},{32,36}... | collective-permute-start | bytes 442376 | tf_op jit(solution)/shard_map/ppermute | solution.py:24
  143.6 6.9 %collective-permute-start.5 = (f32[4,9,8,128]{3,2,1,0:T(8,128)S(1)}, f32[4,9,8,128]{3,2,1,0:T(8,128)S(1)}, u32[]{:S(2)}, u32[]{:S(2)}) collective-permute-start(f32[4,9,8,128]{3,2,1,0:T(8,128)S(1)} %bitcast.76), channel_id=1, source_target_pairs={{0,60},{4,0},{8,4},{12,8},{16,12},{20,16},{24,20},{28,24},{32,28},... | collective-permute-start | bytes 442376 | tf_op jit(solution)/shard_map/ppermute | solution.py:24
  151.4 3.4 %collective-permute-start.7 = (f32[9,8,128]{2,1,0:T(8,128)S(1)}, f32[9,8,128]{2,1,0:T(8,128)S(1)}, u32[]{:S(2)}, u32[]{:S(2)}) collective-permute-start(f32[9,8,128]{2,1,0:T(8,128)S(1)} %get-tuple-element.16.first_ref), channel_id=1, source_target_pairs={{0,448},{64,0},{128,64},{192,128},{256,192},{320,256},{384,320},{4... | collective-permute-start | bytes 110600 | tf_op jit(solution)/shard_map/ppermute | solution.py:24
  153.1 1.8 collective-permute-start.6

commit v3 on v2

--- a/solution.py
+++ b/solution.py
@@ -1,3 +1,5 @@
+import functools
+
 import jax
 import jax.numpy as jnp
 from jax import lax
@@ -47,7 +49,7 @@
         last_ref[f] = columns[120:128]
         return carry
 
-    lax.fori_loop(0, fields, one_field, 0)
+    lax.fori_loop(0, fields, one_field, 0, unroll=3)
 
 
 def inside_rows(place_ref, shape, axis):
@@ -91,33 +93,75 @@
     near_ref[...] = near
 
 
-def field_passes(inside, x, near, far):
-    total = x.shape[0]
-    lane = lax.broadcasted_iota(jnp.int32, (total, 128), 1)
-    left_edge = lane == 0
-    right_edge = lane == 127
-    blank = jnp.zeros((16, 128), jnp.float32)
+def field_passes(coefficients, x, near, far):
+    planes = len(x) // 2
+    lane = lax.broadcasted_iota(jnp.int32, (8, 128), 1)
+    sub = lax.broadcasted_iota(jnp.int32, (8, 128), 0)
+    left_edge, right_edge = lane == 0, lane == 127
+    first_row, last_row = sub == 0, sub == 7
     edges = jnp.concatenate([near, jnp.zeros((112, 128), jnp.float32), far], axis=0).T
-    x = x * inside
     for step in range(4):
-        edge = edges if step == 0 else pltpu.roll(edges, 128 - 2 * step, 1)
-        beside = jnp.where(left_edge, edge, pltpu.roll(x, 1, 1)) + jnp.where(
-            right_edge, edge, pltpu.roll(x, 127, 1)
+        result = []
+        for p in range(planes):
+            top, bottom = x[2 * p], x[2 * p + 1]
+            top_down, bottom_down = pltpu.roll(top, 1, 0), pltpu.roll(bottom, 1, 0)
+            top_up, bottom_up = pltpu.roll(top, 7, 0), pltpu.roll(bottom, 7, 0)
+            across = (
+                top_down + jnp.where(last_row, bottom_up, top_up),
+                jnp.where(first_row, top_down, bottom_down) + bottom_up,
+            )
+            for h in range(2):
+                here = x[2 * p + h]
+                centre, lon_part, lat_part, lev_part = coefficients[h]
+                start = (2 * p + h) * 8
+                edge = edges[start : start + 8]
+                if step:
+                    edge = pltpu.roll(edge, 128 - 2 * step, 1)
+                beside = jnp.where(left_edge, edge, pltpu.roll(here, 1, 1)) + jnp.where(
+                    right_edge, edge, pltpu.roll(here, 127, 1)
+                )
+                total = centre * here + lon_part * beside + lat_part * across[h]
+                if p == 0:
+                    total = total + lev_part * x[2 + h]
+                elif p == planes - 1:
+                    total = total + lev_part * x[2 * p - 2 + h]
+                else:
+                    total = total + lev_part * (x[2 * p - 2 + h] + x[2 * p + 2 + h])
+                result.append(total)
+        x = result
+    return x
+
+
+def coefficients_of(place_ref):
+    halves = []
+    for h in range(2):
+        row = lax.broadcasted_iota(jnp.int32, (8, 128), 0) + 8 * h
+        low = jnp.where(place_ref[0] == 0, HALO, 0)
+        high = jnp.where(place_ref[0] == place_ref[1] - 1, 16 - HALO, 16)
+        inside = jnp.where((row >= low) & (row < high), 1.0, 0.0).astype(jnp.float32)
+        halves.append(
+            (inside * centre_part, inside * spread_lon, inside * spread_lat, inside * spread_lev)
         )
-        across = pltpu.roll(x, 1, 0) + pltpu.roll(x, total - 1, 0)
-        above = jnp.concatenate([x[16:], blank], axis=0)
-        below = jnp.concatenate([blank, x[: total - 16]], axis=0)
-        result = centre_part * x + spread_lon * beside
-        result = result + spread_lat * across
-        result = result + spread_lev * (above + below)
-        x = result * inside
-    return x
+    return halves
+
+
+def field_rows(place_ref, full_ref, f):
+    rows = []
+    for q in range(full_ref.shape[0]):
+        for j in range(full_ref.shape[2]):
+            for h in range(2):
+                row = lax.broadcasted_iota(jnp.int32, (8, 128), 0) + 8 * h
+                low = jnp.where(place_ref[0] == 0, HALO, 0)
+                high = jnp.where(place_ref[0] == place_ref[1] - 1, 16 - HALO, 16)
+                kept = full_ref[q, f, j, 8 * h : 8 * h + 8]
+                rows.append(jnp.where((row >= low) & (row < high), kept, 0.0))
+    return rows
 
 
 def middle_rows(x, plane):
     sub = lax.broadcasted_iota(jnp.int32, (8, 128), 0)
-    top = pltpu.roll(x[plane * 16 : plane * 16 + 8], 4, 0)
-    bottom = pltpu.roll(x[plane * 16 + 8 : plane * 16 + 16], 4, 0)
+    top = pltpu.roll(x[2 * plane], 4, 0)
+    bottom = pltpu.roll(x[2 * plane + 1], 4, 0)
     return jnp.where(sub < 4, top, bottom)
 
 
@@ -125,19 +169,18 @@
     place_ref, full_ref, first_ref, last_ref, west_ref, east_ref, out_ref, near_ref, far_ref
 ):
     groups, fields, planes = full_ref.shape[:3]
-    total = groups * planes * 16
     strip_passes(place_ref, first_ref, last_ref, west_ref, east_ref, near_ref, far_ref)
-    inside = inside_rows(place_ref, (total, 128), 0)
+    coefficients = coefficients_of(place_ref)
 
     def one_field(f, carry):
-        x = full_ref[:, f].reshape(total, 128)
-        x = field_passes(inside, x, near_ref[f], far_ref[f])
+        x = field_rows(place_ref, full_ref, f)
+        x = field_passes(coefficients, x, near_ref[f], far_ref[f])
         for q in range(groups):
             for j in range(planes):
                 out_ref[q, f, j] = middle_rows(x, q * planes + j)
         return carry
 
-    lax.fori_loop(0, fields, one_field, 0)
+    lax.fori_loop(0, fields, one_field, 0, unroll=3)
 
 
 def image_kernel(
@@ -147,23 +190,23 @@
     last_ref,
     west_ref,
     east_ref,
+    direction_ref,
     pair_ref,
     out_ref,
     near_ref,
     far_ref,
 ):
     groups, fields, planes = full_ref.shape[:3]
-    total = groups * planes * 16
     strip_passes(place_ref, first_ref, last_ref, west_ref, east_ref, near_ref, far_ref)
-    inside = inside_rows(place_ref, (total, 128), 0)
+    coefficients = coefficients_of(place_ref)
 
     def one_field(f, sums):
-        x = full_ref[:, f].reshape(total, 128)
-        x = field_passes(inside, x, near_ref[f], far_ref[f])
+        x = field_rows(place_ref, full_ref, f)
+        x = field_passes(coefficients, x, near_ref[f], far_ref[f])
         start_norm, curvature, crossed, squared = sums
         for q in range(groups):
             for j in range(planes):
-                direction = pair_ref[q, f, j]
+                direction = direction_ref[q, f, j]
                 residual = pair_ref[q, fields + f, j]
                 image = direction + middle_rows(x, q * planes + j)
                 out_ref[q, f, j] = image
@@ -174,7 +217,7 @@
         return (start_norm, curvature, crossed, squared)
 
     zero = jnp.zeros((8, 128), jnp.float32)
-    sums = lax.fori_loop(0, fields, one_field, (zero, zero, zero, zero))
+    sums = lax.fori_loop(0, fields, one_field, (zero, zero, zero, zero), unroll=3)
     lane = lax.broadcasted_iota(jnp.int32, (8, 128), 1)
     row = zero
     for k in range(4):
@@ -222,7 +265,59 @@
                 new_direction_ref[q, f, j] = new_residual + ratio * direction
         return carry
 
-    lax.fori_loop(0, fields, one_field, 0)
+    lax.fori_loop(0, fields, one_field, 0, unroll=3)
+
+
+def tiles_kernel(scales, smoothed_ref, ensemble_ref, static_sd_ref, chosen_ref, out_ref):
+    members, variables, planes = ensemble_ref.shape[:3]
+    scale_ens, scale_static = scales
+    tiles = []
+    for v in range(variables):
+        for j in range(planes):
+            parts = []
+            for k in range(members):
+                part = ensemble_ref[k, v, j].astype(jnp.float32) * smoothed_ref[k, j]
+                if k < 4:
+                    parts.append(part)
+                else:
+                    parts[k % 4] = parts[k % 4] + part
+            ens_part = (parts[0] + parts[1]) + (parts[2] + parts[3])
+            static = static_sd_ref[v, j] * smoothed_ref[members + v, j]
+            tiles.append(scale_ens * ens_part + scale_static * static)
+    tiles = jnp.concatenate(tiles, axis=0).astype(jnp.bfloat16)
+    picked = jnp.dot(chosen_ref[...], tiles, preferred_element_type=jnp.float32)
+    out_ref[...] = picked.astype(jnp.bfloat16)
+
+
+def back_kernel(
+    scales, came_back_ref, chosen_ref, ensemble_ref, static_sd_ref, residual_ref, out_ref
+):
+    members, variables, planes = ensemble_ref.shape[:3]
+    share = out_ref.shape[1] // 2
+    scale_ens, scale_static = scales
+    adjoint = lax.dot_general(
+        chosen_ref[...],
+        came_back_ref[...],
+        (((0,), (0,)), ((), ())),
+        preferred_element_type=jnp.float32,
+    )
+
+    def part(v, j):
+        start = (v * planes + j) * 8
+        return adjoint[start : start + 8]
+
+    for k in range(members + variables):
+        q, f = divmod(k, share)
+        for j in range(planes):
+            if k < members:
+                total = ensemble_ref[k, 0, j].astype(jnp.float32) * part(0, j)
+                for v in range(1, variables):
+                    total = total + ensemble_ref[k, v, j].astype(jnp.float32) * part(v, j)
+                out_ref[q, f, j] = scale_ens * total
+            else:
+                v = k - members
+                out_ref[q, f, j] = scale_static * static_sd_ref[v, j] * part(v, j)
+            out_ref[q, share + f, j] = residual_ref[k, j]
 
 
 def swap_lev(blocks):
@@ -268,7 +363,7 @@
         return local_call(smooth_kernel, out, 1, "smooth", scratch)(*operands)
     shape[1] += 1
     out = jax.ShapeDtypeStruct(tuple(shape), jnp.float32)
-    return local_call(image_kernel, out, 1, "image", scratch)(*operands, tail)
+    return local_call(image_kernel, out, 1, "image", scratch)(*operands, *tail)
 
 
 def body(
@@ -292,23 +387,24 @@
     groups = lax.axis_size("lev")
     share = direction.shape[0] // groups
     grouped = (groups, share, levels, lat_rows, lon_cells)
-    pair = swap_lev(
-        jnp.concatenate([direction.reshape(grouped), residual.reshape(grouped)], axis=1)
-    )
-    smoothed = swap_lev(smooth(pair, share)).reshape(direction.shape)
-    ens_part = jnp.sum(ensemble * smoothed[:members, None], axis=0)
-    increment = (scale_ens * ens_part + static_part * static_sd * smoothed[members:]).astype(
-        jnp.bfloat16
-    )
-    tile_table = increment.transpose(1, 2, 0, 3).reshape(tile_total, tile_width)
-    tile_pick = send_tile.reshape(group_size * slot_count)
+    direction_blocks = swap_lev(direction.reshape(grouped))
+    smoothed = swap_lev(smooth(direction_blocks, share)).reshape(direction.shape)
+    tile_pick = send_tile.reshape(group_size, 1, slot_count)
     is_live = (
         jnp.arange(slot_count, dtype=jnp.int32)[None, :] < pair_count.reshape(group_size)[:, None]
     )
-    outgoing = jnp.take(tile_table, tile_pick, axis=0)
-    outgoing = jnp.where(
-        is_live.reshape(group_size * slot_count)[:, None], outgoing, jnp.zeros_like(outgoing)
-    )
+    row_pick = jnp.arange(variables, dtype=jnp.int32)[None, :, None] * tile_total + tile_pick
+    row_pick = jnp.where(is_live[:, None, :], row_pick, -1)
+    row_pick = row_pick.reshape(group_size * variables * slot_count)
+    chosen = row_pick[:, None] == jnp.arange(variables * tile_total, dtype=jnp.int32)[None, :]
+    chosen = chosen.astype(jnp.bfloat16)
+    scales = (scale_ens, static_part)
+    rows = jax.ShapeDtypeStruct((group_size * variables * slot_count, lon_cells), jnp.bfloat16)
+    outgoing = local_call(functools.partial(tiles_kernel, scales), rows, 0, "tiles")(
+        smoothed, ensemble, static_sd, chosen
+    )
+    block_shape = (group_size, variables, slot_count, lon_cells)
+    outgoing = outgoing.reshape(block_shape).transpose(0, 2, 1, 3)
     outgoing = outgoing.reshape(group_size, slot_count, tile_width)
     arrived = lax.all_to_all(outgoing, LON_LAT, split_axis=0, concat_axis=0, tiled=True)
     weights = obs_weight.reshape(group_size, slot_count, obs_count, tile_width)
@@ -319,16 +415,14 @@
     returned = jnp.einsum("gsbc,gsb->gsc", weights, weighted, preferred_element_type=jnp.float32)
     returned = returned.astype(jnp.bfloat16)
     came_back = lax.all_to_all(returned, LON_LAT, split_axis=0, concat_axis=0, tiled=True)
-    came_back = came_back.reshape(group_size * slot_count, tile_width)
-    one_hot = (tile_pick[:, None] == jnp.arange(tile_total, dtype=jnp.int32)[None, :]).astype(
-        jnp.bfloat16
-    )
-    adj_tiles = jnp.dot(one_hot.T, came_back, preferred_element_type=jnp.float32)
-    adjoint = adj_tiles.reshape(levels, lat_rows, variables, lon_cells).transpose(2, 0, 1, 3)
-    back_ens = scale_ens * jnp.sum(ensemble * adjoint[None], axis=1)
-    back_static = static_part * static_sd * adjoint
-    back = jnp.concatenate([back_ens, back_static], axis=0)
-    image = swap_lev(smooth(swap_lev(back.reshape(grouped)), share, pair))
+    came_back = came_back.reshape(group_size, slot_count, variables, lon_cells)
+    came_back = came_back.transpose(0, 2, 1, 3).reshape(-1, lon_cells)
+    paired = jax.ShapeDtypeStruct((groups, 2 * share, levels, lat_rows, lon_cells), jnp.float32)
+    pair = local_call(functools.partial(back_kernel, scales), paired, 0, "back")(
+        came_back, chosen, ensemble, static_sd, residual
+    )
+    pair = swap_lev(pair)
+    image = swap_lev(smooth(pair, share, (direction_blocks, pair)))
     peers = lax.axis_size(LON_LAT)
     row = jnp.sum(image[:, share, 0, 0, :], axis=0)
     rows = lax.all_to_all(

time: 196 us -> 187 us (0.954)
  blocking collectives: 83.8 us -> 116 us
  waiting for transfers between devices: 41.3 us -> 15.7 us
  starting transfers between devices: 41.3 us -> 34.2 us
  local copies, waits for them, and re-layouts: 7.31 us -> 3.3 us
  other arithmetic: 5.53 us -> 1.89 us
    all_to_all x0 -> x1, blocking collectives: none -> 28.6 us  [body(): lax.all_to_all(returned, LON_LAT, split_axis=0, concat_axis=0, tiled=True)]
    all_to_all x1 -> x0, waiting for transfers between devices: 22.9 us -> none  [body(): lax.all_to_all(returned, LON_LAT, split_axis=0, concat_axis=0, tiled=True)]
    all_to_all x1 -> x0, starting transfers between devices: 5.73 us -> none  [body(): lax.all_to_all(returned, LON_LAT, split_axis=0, concat_axis=0, tiled=True)]
    all_to_all x2, blocking collectives: 18.3 us -> 21.3 us  [swap_lev(): lax.all_to_all(blocks, 'lev', split_axis=0, concat_axis=0, tiled=True)]
    all_to_all x2, waiting for transfers between devices: 11.9 us -> 9.63 us  [swap_lev(): lax.all_to_all(blocks, 'lev', split_axis=0, concat_axis=0, tiled=True)]
    concatenate x2 -> x0, other arithmetic: 2.11 us -> none  [the longest x1 2.08 us: body(): jnp.concatenate([direction.reshape(grouped), residual.reshape(grouped)],...]
    pallas_call x5 -> x7, Pallas kernels: 12.8 us -> 12 us  [run(): pl.pallas_call(kernel, out_shape=out_shape, in_specs=in_specs, out_specs=...]
  transfers between devices with their start and end apart: 11 -> 10, of which waited for: 8 -> 7; matrix products, arithmetic and copies ran while one was open for 1% -> 2% of each run, Pallas kernels for 0% -> 0%
where the time goes in v3:
time: 187 us; the launch traced here: 186 us
  blocking collectives  116 us (62%)
  starting transfers between devices  34.2 us (18%)
  waiting for transfers between devices  15.7 us (8%)
  Pallas kernels  12 us (6%)
  local copies, waits for them, and re-layouts  3.3 us (2%)
  matrix products  2.57 us (1%)
  other arithmetic  1.89 us (1%)
    all_to_all x1, blocking collectives, body(): lax.all_to_all(outgoing, LON_LAT, split_axis=0, concat_axis=0, tiled=True)  38.8 us
    all_to_all x1, blocking collectives, body(): lax.all_to_all(returned, LON_LAT, split_axis=0, concat_axis=0, tiled=True)  28.6 us
    all_to_all x1, blocking collectives, body(): lax.all_to_all(jnp.broadcast_to(row, (peers, 1, lon_cells)), LON_LAT, spl...  26.7 us
    ppermute x8, starting transfers between devices, shift(): lax.ppermute(x, axis, [(i, (i + step) % devices) for i in range(devices)])  25.7 us
    all_to_all x2, blocking collectives, swap_lev(): lax.all_to_all(blocks, 'lev', split_axis=0, concat_axis=0, tiled=True)  21.3 us
    pallas_call x7, Pallas kernels, run(): pl.pallas_call(kernel, out_shape=out_shape, in_specs=in_specs, out_specs=...  12 us
    all_to_all x2, waiting for transfers between devices, swap_lev(): lax.all_to_all(blocks, 'lev', split_axis=0, concat_axis=0, tiled=True)  9.63 us
    all_to_all x2, starting transfers between devices, swap_lev(): lax.all_to_all(blocks, 'lev', split_axis=0, concat_axis=0, tiled=True)  8.6 us
  transfers between devices with their start and end apart: 10, of which 7 were waited for; matrix products, arithmetic and copies ran while one was open for 2% of the time, Pallas kernels for 0%

profile of v3, /device:TPU:1, one launch (start us, length us, event | category | flops | bytes accessed | tf_op | source)
XLA Modules:
  0.0 186.0 jit_solution(12019701386725677998)
XLA Ops:
  0.7 5.1 %all-to-all-start = ((f32[4,9,2,8,128]{4,3,2,1,0:T(8,128)}), f32[4,9,2,8,128]{4,3,2,1,0:T(8,128)S(1)}, u32[]{:S(2)}, u32[]{:S(2)}) async-start(f32[4,9,2,8,128]{4,3,2,1,0:T(8,128)} %bitcast.47), calls=%async_computation | async-start | bytes 589824 | tf_op jit(solution)/shard_map/all_to_all | solution.py:324
  7.3 4.2 %all-to-all-done.own_ref.direction_ref = f32[4,9,2,8,128]{4,3,2,1,0:T(8,128)S(1)} async-done(((f32[4,9,2,8,128]{4,3,2,1,0:T(8,128)}), f32[4,9,2,8,128]{4,3,2,1,0:T(8,128)S(1)}, u32[]{:S(2)}, u32[]{:S(2)}) %all-to-all-start) | async-done | bytes 294944 | tf_op jit(solution)/shard_map/all_to_all | solution.py:324
  11.6 3.7 %collective-permute-start = (f32[4,9,8,128]{3,2,1,0:T(8,128)S(1)}, f32[4,9,8,128]{3,2,1,0:T(8,128)S(1)}, u32[]{:S(2)}, u32[]{:S(2)}) collective-permute-start(f32[4,9,8,128]{3,2,1,0:T(8,128)S(1)} %bitcast.58), channel_id=1, source_target_pairs={{0,4},{4,8},{8,12},{12,16},{16,20},{20,24},{24,28},{28,32},{32,36}... | collective-permute-start | bytes 442376 | tf_op jit(solution)/shard_map/ppermute | solution.py:26
  15.3 9.5 %collective-permute-start.1 = (f32[4,9,8,128]{3,2,1,0:T(8,128)S(1)}, f32[4,9,8,128]{3,2,1,0:T(8,128)S(1)}, u32[]{:S(2)}, u32[]{:S(2)}) collective-permute-start(f32[4,9,8,128]{3,2,1,0:T(8,128)S(1)} %bitcast.57), channel_id=1, source_target_pairs={{0,60},{4,0},{8,4},{12,8},{16,12},{20,16},{24,20},{28,24},{32,28},... | collective-permute-start | bytes 442376 | tf_op jit(solution)/shard_map/ppermute | solution.py:26
  25.6 1.2 collective-permute-done.1.south_ref
  27.9 3.0 %collective-permute-start.3 = (f32[9,8,128]{2,1,0:T(8,128)}, f32[9,8,128]{2,1,0:T(8,128)}, u32[]{:S(2)}, u32[]{:S(2)}) collective-permute-start(f32[9,8,128]{2,1,0:T(8,128)} %get-tuple-element.13.first_ref), channel_id=1, source_target_pairs={{0,448},{64,0},{128,64},{192,128},{256,192},{320,256},{384,320},{4... | collective-permute-start | bytes 110600 | tf_op jit(solution)/shard_map/ppermute | solution.py:26
  30.9 1.1 collective-permute-start.2
  32.0 1.2 select_n.12
  33.9 4.8 %smooth.1 = f32[4,9,2,8,128]{4,3,2,1,0:T(8,128)} custom-call(s32[2]{0:T(128)S(1)} %pad_add_fusion.place_ref, f32[4,9,2,16,128]{4,3,2,1,0:T(8,128)S(1)} %get-tuple-element.12.full_ref, f32[9,8,128]{2,1,0:T(8,128)} %get-tuple-element.13.first_ref, f32[9,8,128]{2,1,0:T(8,128)} %get-tuple-element.14.last_ref, f32[9,8,128]{2,1,0:T(8,128)} %collective-permute-done.2.west_ref, ...), custom_call_target="tpu_custom_call" | custom-call | tf_op jit(solution)/shard_map/smooth/pallas_call | solution.py:331
  38.7 3.5 %all-to-all-start.1 = ((f32[4,9,2,8,128]{4,3,2,1,0:T(8,128)}), f32[4,9,2,8,128]{4,3,2,1,0:T(8,128)S(1)}, u32[]{:S(2)}, u32[]{:S(2)}) async-start(f32[4,9,2,8,128]{4,3,2,1,0:T(8,128)} %smooth.1), calls=%async_computation.1 | async-start | bytes 589824 | tf_op jit(solution)/shard_map/all_to_all | solution.py:324
  42.4 5.5 %all-to-all-done.1 = f32[4,9,2,8,128]{4,3,2,1,0:T(8,128)S(1)} async-done(((f32[4,9,2,8,128]{4,3,2,1,0:T(8,128)}), f32[4,9,2,8,128]{4,3,2,1,0:T(8,128)S(1)}, u32[]{:S(2)}, u32[]{:S(2)}) %all-to-all-start.1) | async-done | bytes 294944 | tf_op jit(solution)/shard_map/all_to_all | solution.py:324
  48.2 38.8 %all_to_all.35 = bf16[128,2,512]{2,1,0:T(2,128)(2,1)S(1)} all-to-all(bf16[128,2,512]{2,1,0:T(2,128)(2,1)S(1)} %bitcast.52), channel_id=1, replica_groups=mesh['lon_0'=4,'lon_1'=2,'lat'=16,'lev'=4] {'lon_0','lon_1','lat'}, dimensions={0} | all-to-all | bytes 524288 | tf_op jit(solution)/shard_map/all_to_all | solution.py:409
  88.9 1.6 fusion
  90.8 28.6 %all_to_all.36 = bf16[128,2,512]{2,1,0:T(2,128)(2,1)S(1)} all-to-all(bf16[128,2,512]{2,1,0:T(2,128)(2,1)S(1)} %bitcast.55), channel_id=1, replica_groups=mesh['lon_0'=4,'lon_1'=2,'lat'=16,'lev'=4] {'lon_0','lon_1','lat'}, dimensions={0} | all-to-all | bytes 524288 | tf_op jit(solution)/shard_map/all_to_all | solution.py:417
  119.8 13.1 %all_to_all.37.own_ref.pair_ref = f32[4,18,2,8,128]{4,3,2,1,0:T(8,128)S(1)} all-to-all(f32[4,18,2,8,128]{4,3,2,1,0:T(8,128)S(1)} %back.1), channel_id=1, replica_groups=mesh['lon_0'=4,'lon_1'=2,'lat'=16,'lev'=4] {'lev'}, dimensions={0} | all-to-all | bytes 1179648 | tf_op jit(solution)/shard_map/all_to_all | solution.py:324
  132.9 2.5 %collective-permute-start.4 = (f32[4,9,8,128]{3,2,1,0:T(8,128)S(1)}, f32[4,9,8,128]{3,2,1,0:T(8,128)S(1)}, u32[]{:S(2)}, u32[]{:S(2)}) collective-permute-start(f32[4,9,8,128]{3,2,1,0:T(8,128)S(1)} %bitcast.60), channel_id=1, source_target_pairs={{0,4},{4,8},{8,12},{12,16},{16,20},{20,24},{24,28},{28,32},{32,36}... | collective-permute-start | bytes 442376 | tf_op jit(solution)/shard_map/ppermute | solution.py:26
  135.4 4.1 %collective-permute-start.5 = (f32[4,9,8,128]{3,2,1,0:T(8,128)S(1)}, f32[4,9,8,128]{3,2,1,0:T(8,128)S(1)}, u32[]{:S(2)}, u32[]{:S(2)}) collective-permute-start(f32[4,9,8,128]{3,2,1,0:T(8,128)S(1)} %bitcast.59), channel_id=1, source_target_pairs={{0,60},{4,0},{8,4},{12,8},{16,12},{20,16},{24,20},{28,24},{32,28},... | collective-permute-start | bytes 442376 | tf_op jit(solution)/shard_map/ppermute | solution.py:26
  139.6 1.6 collective-permute-done.4.north_ref
  142.5 1.6 collective-permute-start.7
  144.2 1.6 collective-permute-done.7.east_ref
  145.9 4.0 %image.1 = f32[4,10,2,8,128]{4,3,2,1,0:T(8,128)S(1)} custom-call(s32[2]{0:T(128)S(1)} %pad_add_fusion.place_ref, f32[4,9,2,16,128]{4,3,2,1,0:T(8,128)S(1)} %get-tuple-element.15.full_ref, f32[9,8,128]{2,1,0:T(8,128)S(1)} %get-tuple-element.16.first_ref, f32[9,8,128]{2,1,0:T(8,128)S(1)} %get-tuple-element.17.last_ref, ...), custom_call_target="tpu_custom_call" | custom-call | tf_op jit(solution)/shard_map/image/pallas_call | solution.py:331
  149.8 8.2 %all_to_all.38.image_ref = f32[4,10,2,8,128]{4,3,2,1,0:T(8,128)S(1)} all-to-all(f32[4,10,2,8,128]{4,3,2,1,0:T(8,128)S(1)} %image.1), channel_id=1, replica_groups=mesh['lon_0'=4,'lon_1'=2,'lat'=16,'lev'=4] {'lev'}, dimensions={0} | all-to-all | bytes 655360 | tf_op jit(solution)/shard_map/all_to_all | solution.py:324
  158.1 26.7 %all_to_all.39 = f32[128,1,128]{2,1,0:T(1,128)S(1)} all-to-all(f32[128,1,128]{2,1,0:T(1,128)S(1)} %broadcast_in_dim.21), channel_id=1, replica_groups=mesh['lon_0'=4,'lon_1'=2,'lat'=16,'lev'=4] {'lon_0','lon_1','lat'}, dimensions={0} | all-to-all | bytes 131072 | tf_op jit(solution)/shard_map/all_to_all | solution.py:428
  184.9 1.1 update.1
  (39 shorter events, 8.8 us)
Async XLA Ops:
  0.6 86.4 %copy-start = (bf16[1,1,1,128,2,8,512]{6,5,4,3,2,1,0:T(8,128)(2,1)S(1)}, bf16[1,1,1,128,2,8,512]{6,5,4,3,2,1,0:T(8,128)(2,1)}, u32[]{:S(2)}) copy-start(bf16[1,1,1,128,2,8,512]{6,5,4,3,2,1,0:T(8,128)(2,1)} %param.16) | copy-start | bytes 6291460
  0.6 47.2 %copy-start.1 = (bf16[32,4,2,8,128]{4,3,2,1,0:T(8,128)(2,1)S(1)}, bf16[32,4,2,8,128]{4,3,2,1,0:T(8,128)(2,1)}, u32[]{:S(2)}) copy-start(bf16[32,4,2,8,128]{4,3,2,1,0:T(8,128)(2,1)} %ensemble_ref.3) | copy-start | bytes 1572868
  0.7 47.2 %copy-start.5 = (f32[4,2,8,128]{3,2,1,0:T(8,128)S(1)}, f32[4,2,8,128]{3,2,1,0:T(8,128)}, u32[]{:S(2)}) copy-start(f32[4,2,8,128]{3,2,1,0:T(8,128)} %static_sd_ref.3) | copy-start | bytes 98308
  0.7 10.8 %all-to-all-start = ((f32[4,9,2,8,128]{4,3,2,1,0:T(8,128)}), f32[4,9,2,8,128]{4,3,2,1,0:T(8,128)S(1)}, u32[]{:S(2)}, u32[]{:S(2)}) async-start(f32[4,9,2,8,128]{4,3,2,1,0:T(8,128)} %bitcast.47), calls=%async_computation | async-start | bytes 589824 | tf_op jit(solution)/shard_map/all_to_all | solution.py:324
  11.6 14.1 %collective-permute-start = (f32[4,9,8,128]{3,2,1,0:T(8,128)S(1)}, f32[4,9,8,128]{3,2,1,0:T(8,128)S(1)}, u32[]{:S(2)}, u32[]{:S(2)}) collective-permute-start(f32[4,9,8,128]{3,2,1,0:T(8,128)S(1)} %bitcast.58), channel_id=1, source_target_pairs={{0,4},{4,8},{8,12},{12,16},{16,20},{20,24},{24,28},{28,32},{32,36}... | collective-permute-start | bytes 442376 | tf_op jit(solution)/shard_map/ppermute | solution.py:26
  15.3 11.6 %collective-permute-start.1 = (f32[4,9,8,128]{3,2,1,0:T(8,128)S(1)}, f32[4,9,8,128]{3,2,1,0:T(8,128)S(1)}, u32[]{:S(2)}, u32[]{:S(2)}) collective-permute-start(f32[4,9,8,128]{3,2,1,0:T(8,128)S(1)} %bitcast.57), channel_id=1, source_target_pairs={{0,60},{4,0},{8,4},{12,8},{16,12},{20,16},{24,20},{28,24},{32,28},... | collective-permute-start | bytes 442376 | tf_op jit(solution)/shard_map/ppermute | solution.py:26
  27.9 6.0 %collective-permute-start.3 = (f32[9,8,128]{2,1,0:T(8,128)}, f32[9,8,128]{2,1,0:T(8,128)}, u32[]{:S(2)}, u32[]{:S(2)}) collective-permute-start(f32[9,8,128]{2,1,0:T(8,128)} %get-tuple-element.13.first_ref), channel_id=1, source_target_pairs={{0,448},{64,0},{128,64},{192,128},{256,192},{320,256},{384,320},{4... | collective-permute-start | bytes 110600 | tf_op jit(solution)/shard_map/ppermute | solution.py:26
  30.9 3.1 %collective-permute-start.2 = (f32[9,8,128]{2,1,0:T(8,128)}, f32[9,8,128]{2,1,0:T(8,128)}, u32[]{:S(2)}, u32[]{:S(2)}) collective-permute-start(f32[9,8,128]{2,1,0:T(8,128)} %get-tuple-element.14.last_ref), channel_id=1, source_target_pairs={{0,64},{64,128},{128,192},{192,256},{256,320},{320,384},{384,448},... | collective-permute-start | bytes 110600 | tf_op jit(solution)/shard_map/ppermute | solution.py:26
  38.7 9.1 %all-to-all-start.1 = ((f32[4,9,2,8,128]{4,3,2,1,0:T(8,128)}), f32[4,9,2,8,128]{4,3,2,1,0:T(8,128)S(1)}, u32[]{:S(2)}, u32[]{:S(2)}) async-start(f32[4,9,2,8,128]{4,3,2,1,0:T(8,128)} %smooth.1), calls=%async_computation.1 | async-start | bytes 589824 | tf_op jit(solution)/shard_map/all_to_all | solution.py:324
  87.0 1.1 copy-start.6
  88.1 31.3 %copy-start.3 = (f32[36,2,8,128]{3,2,1,0:T(8,128)S(1)}, f32[36,2,8,128]{3,2,1,0:T(8,128)}, u32[]{:S(2)}) copy-start(f32[36,2,8,128]{3,2,1,0:T(8,128)} %residual_ref.1) | copy-start | bytes 884740
  132.9 52.0 %copy-start.2 = (f32[36,2,8,128]{3,2,1,0:T(8,128)S(1)}, f32[36,2,8,128]{3,2,1,0:T(8,128)}, u32[]{:S(2)}) copy-start(f32[36,2,8,128]{3,2,1,0:T(8,128)} %param.11) | copy-start | bytes 884740
  132.9 52.0 %copy-start.4 = (f32[36,2,8,128]{3,2,1,0:T(8,128)S(1)}, f32[36,2,8,128]{3,2,1,0:T(8,128)}, u32[]{:S(2)}) copy-start(f32[36,2,8,128]{3,2,1,0:T(8,128)} %param.9) | copy-start | bytes 884740
  132.9 8.2 %collective-permute-start.4 = (f32[4,9,8,128]{3,2,1,0:T(8,128)S(1)}, f32[4,9,8,128]{3,2,1,0:T(8,128)S(1)}, u32[]{:S(2)}, u32[]{:S(2)}) collective-permute-start(f32[4,9,8,128]{3,2,1,0:T(8,128)S(1)} %bitcast.60), channel_id=1, source_target_pairs={{0,4},{4,8},{8,12},{12,16},{16,20},{20,24},{24,28},{28,32},{32,36}... | collective-permute-start | bytes 442376 | tf_op jit(solution)/shard_map/ppermute | solution.py:26
  135.4 6.6 %collective-permute-start.5 = (f32[4,9,8,128]{3,2,1,0:T(8,128)S(1)}, f32[4,9,8,128]{3,2,1,0:T(8,128)S(1)}, u32[]{:S(2)}, u32[]{:S(2)}) collective-permute-start(f32[4,9,8,128]{3,2,1,0:T(8,128)S(1)} %bitcast.59), channel_id=1, source_target_pairs={{0,60},{4,0},{8,4},{12,8},{16,12},{20,16},{24,20},{28,24},{32,28},... | collective-permute-start | bytes 442376 | tf_op jit(solution)/shard_map/ppermute | solution.py:26
  142.5 3.4 %collective-permute-start.7 = (f32[9,8,128]{2,1,0:T(8,128)S(1)}, f32[9,8,128]{2,1,0:T(8,128)S(1)}, u32[]{:S(2)}, u32[]{:S(2)}) collective-permute-start(f32[9,8,128]{2,1,0:T(8,128)S(1)} %get-tuple-element.16.first_ref), channel_id=1, source_target_pairs={{0,448},{64,0},{128,64},{192,128},{256,192},{320,256},{384,320},{4... | collective-permute-start | bytes 110600 | tf_op jit(solution)/shard_map/ppermute | solution.py:26
  144.1 1.8 collective-permute-start.6

commit v4 on v3

--- a/solution.py
+++ b/solution.py
@@ -33,10 +33,10 @@
     def one_field(f, carry):
         rows = []
         for q in range(groups):
-            north = north_ref[q, f]
-            south = south_ref[q, f]
+            north = north_ref[q, f].astype(jnp.float32)
+            south = south_ref[q, f].astype(jnp.float32)
             for j in range(planes):
-                own = pltpu.roll(own_ref[q, f, j], 4, 0)
+                own = pltpu.roll(own_ref[q, f, j].astype(jnp.float32), 4, 0)
                 above = north if j == 0 else pltpu.roll(north, 4, 0)
                 below = pltpu.roll(south, 4, 0) if j == 0 else south
                 top = jnp.where(row < 4, above, own)
@@ -207,7 +207,7 @@
         for q in range(groups):
             for j in range(planes):
                 direction = direction_ref[q, f, j]
-                residual = pair_ref[q, fields + f, j]
+                residual = pair_ref[q, fields + f, j].astype(jnp.float32)
                 image = direction + middle_rows(x, q * planes + j)
                 out_ref[q, f, j] = image
                 start_norm = start_norm + residual * residual
@@ -313,11 +313,12 @@
                 total = ensemble_ref[k, 0, j].astype(jnp.float32) * part(0, j)
                 for v in range(1, variables):
                     total = total + ensemble_ref[k, v, j].astype(jnp.float32) * part(v, j)
-                out_ref[q, f, j] = scale_ens * total
+                out_ref[q, f, j] = (scale_ens * total).astype(jnp.bfloat16)
             else:
                 v = k - members
-                out_ref[q, f, j] = scale_static * static_sd_ref[v, j] * part(v, j)
-            out_ref[q, share + f, j] = residual_ref[k, j]
+                static = scale_static * static_sd_ref[v, j] * part(v, j)
+                out_ref[q, f, j] = static.astype(jnp.bfloat16)
+            out_ref[q, share + f, j] = residual_ref[k, j].astype(jnp.bfloat16)
 
 
 def swap_lev(blocks):
@@ -343,7 +344,7 @@
 
 def smooth(blocks, share, tail=None):
     groups, _, levels, lat_rows, lon_cells = blocks.shape
-    own = blocks[:, :share]
+    own = blocks[:, :share].astype(jnp.bfloat16)
     halo_shape = (groups, share, levels * HALO, lon_cells)
     north = shift(own[..., lat_rows - HALO :, :].reshape(halo_shape), "lat", 1)
     south = shift(own[..., :HALO, :].reshape(halo_shape), "lat", -1)
@@ -417,7 +418,7 @@
     came_back = lax.all_to_all(returned, LON_LAT, split_axis=0, concat_axis=0, tiled=True)
     came_back = came_back.reshape(group_size, slot_count, variables, lon_cells)
     came_back = came_back.transpose(0, 2, 1, 3).reshape(-1, lon_cells)
-    paired = jax.ShapeDtypeStruct((groups, 2 * share, levels, lat_rows, lon_cells), jnp.float32)
+    paired = jax.ShapeDtypeStruct((groups, 2 * share, levels, lat_rows, lon_cells), jnp.bfloat16)
     pair = local_call(functools.partial(back_kernel, scales), paired, 0, "back")(
         came_back, chosen, ensemble, static_sd, residual
     )

time: 187 us -> 186 us (level)
  blocking collectives: 116 us -> 112 us
  local copies, waits for them, and re-layouts: 3.3 us -> 7.23 us
  waiting for transfers between devices: 15.7 us -> 13.3 us
    all_to_all x2, blocking collectives: 21.3 us -> 18.3 us  [swap_lev(): lax.all_to_all(blocks, 'lev', split_axis=0, concat_axis=0, tiled=True)]
    unnamed x14 -> x22, local copies, waits for them, and re-layouts: 0.05 us -> 3.08 us
    ppermute x8, waiting for transfers between devices: 6.06 us -> 3.71 us  [shift(): lax.ppermute(x, axis, [(i, (i + step) % devices) for i in range(devices)])]
  transfers between devices with their start and end apart: 10 -> 10, of which waited for: 7 -> 5; matrix products, arithmetic and copies ran while one was open for 2% -> 2% of each run, Pallas kernels for 0% -> 0%
where the time goes in v4:
time: 186 us; the launch traced here: 185 us
  blocking collectives  112 us (60%)
  starting transfers between devices  34.3 us (18%)
  waiting for transfers between devices  13.3 us (7%)
  Pallas kernels  11.9 us (6%)
  local copies, waits for them, and re-layouts  7.23 us (4%)
  matrix products  3.24 us (2%)
  other arithmetic  1.91 us (1%)
    all_to_all x1, blocking collectives, body(): lax.all_to_all(outgoing, LON_LAT, split_axis=0, concat_axis=0, tiled=True)  38.7 us
    all_to_all x1, blocking collectives, body(): lax.all_to_all(returned, LON_LAT, split_axis=0, concat_axis=0, tiled=True)  28.6 us
    all_to_all x1, blocking collectives, body(): lax.all_to_all(jnp.broadcast_to(row, (peers, 1, lon_cells)), LON_LAT, spl...  26.8 us
    ppermute x8, starting transfers between devices, shift(): lax.ppermute(x, axis, [(i, (i + step) % devices) for i in range(devices)])  25.7 us
    all_to_all x2, blocking collectives, swap_lev(): lax.all_to_all(blocks, 'lev', split_axis=0, concat_axis=0, tiled=True)  18.3 us
    pallas_call x7, Pallas kernels, run(): pl.pallas_call(kernel, out_shape=out_shape, in_specs=in_specs, out_specs=...  11.9 us
    all_to_all x2, waiting for transfers between devices, swap_lev(): lax.all_to_all(blocks, 'lev', split_axis=0, concat_axis=0, tiled=True)  9.63 us
    all_to_all x2, starting transfers between devices, swap_lev(): lax.all_to_all(blocks, 'lev', split_axis=0, concat_axis=0, tiled=True)  8.6 us
  transfers between devices with their start and end apart: 10, of which 5 were waited for; matrix products, arithmetic and copies ran while one was open for 2% of the time, Pallas kernels for 0%

profile of v4, /device:TPU:1, one launch (start us, length us, event | category | flops | bytes accessed | tf_op | source)
XLA Modules:
  0.0 185.2 jit_solution(7361401052171807016)
XLA Ops:
  0.7 5.1 %all-to-all-start = ((f32[4,9,2,8,128]{4,3,2,1,0:T(8,128)}), f32[4,9,2,8,128]{4,3,2,1,0:T(8,128)S(1)}, u32[]{:S(2)}, u32[]{:S(2)}) async-start(f32[4,9,2,8,128]{4,3,2,1,0:T(8,128)} %bitcast.48), calls=%async_computation | async-start | bytes 589824 | tf_op jit(solution)/shard_map/all_to_all | solution.py:325
  7.3 4.2 %all-to-all-done.own_ref.direction_ref = f32[4,9,2,8,128]{4,3,2,1,0:T(8,128)S(1)} async-done(((f32[4,9,2,8,128]{4,3,2,1,0:T(8,128)}), f32[4,9,2,8,128]{4,3,2,1,0:T(8,128)S(1)}, u32[]{:S(2)}, u32[]{:S(2)}) %all-to-all-start) | async-done | bytes 294944 | tf_op jit(solution)/shard_map/all_to_all | solution.py:325
  11.6 3.7 %collective-permute-start = (bf16[4,9,8,128]{3,2,1,0:T(8,128)(2,1)S(1)}, bf16[4,9,8,128]{3,2,1,0:T(8,128)(2,1)S(1)}, u32[]{:S(2)}, u32[]{:S(2)}) collective-permute-start(bf16[4,9,8,128]{3,2,1,0:T(8,128)(2,1)S(1)} %bitcast.58), channel_id=1, source_target_pairs={{0,4},{4,8},{8,12},{12,16},{16,20},{20,24},{24,28},{28,32},{32,36}... | collective-permute-start | bytes 221192 | tf_op jit(solution)/shard_map/ppermute | solution.py:26
  15.3 9.5 %collective-permute-start.1 = (bf16[4,9,8,128]{3,2,1,0:T(8,128)(2,1)S(1)}, bf16[4,9,8,128]{3,2,1,0:T(8,128)(2,1)S(1)}, u32[]{:S(2)}, u32[]{:S(2)}) collective-permute-start(bf16[4,9,8,128]{3,2,1,0:T(8,128)(2,1)S(1)} %bitcast.57), channel_id=1, source_target_pairs={{0,60},{4,0},{8,4},{12,8},{16,12},{20,16},{24,20},{28,24},{32,28},... | collective-permute-start | bytes 221192 | tf_op jit(solution)/shard_map/ppermute | solution.py:26
  29.7 2.9 %collective-permute-start.3 = (f32[9,8,128]{2,1,0:T(8,128)}, f32[9,8,128]{2,1,0:T(8,128)}, u32[]{:S(2)}, u32[]{:S(2)}) collective-permute-start(f32[9,8,128]{2,1,0:T(8,128)} %get-tuple-element.13.first_ref), channel_id=1, source_target_pairs={{0,448},{64,0},{128,64},{192,128},{256,192},{320,256},{384,320},{4... | collective-permute-start | bytes 110600 | tf_op jit(solution)/shard_map/ppermute | solution.py:26
  32.6 1.1 collective-permute-start.2
  33.8 1.2 select_n.12
  35.7 4.8 %smooth.1 = f32[4,9,2,8,128]{4,3,2,1,0:T(8,128)} custom-call(s32[2]{0:T(128)S(1)} %pad_add_fusion.place_ref, f32[4,9,2,16,128]{4,3,2,1,0:T(8,128)S(1)} %get-tuple-element.12.full_ref, f32[9,8,128]{2,1,0:T(8,128)} %get-tuple-element.13.first_ref, f32[9,8,128]{2,1,0:T(8,128)} %get-tuple-element.14.last_ref, f32[9,8,128]{2,1,0:T(8,128)} %collective-permute-done.2.west_ref, ...), custom_call_target="tpu_custom_call" | custom-call | tf_op jit(solution)/shard_map/smooth/pallas_call | solution.py:332
  40.5 3.5 %all-to-all-start.1 = ((f32[4,9,2,8,128]{4,3,2,1,0:T(8,128)}), f32[4,9,2,8,128]{4,3,2,1,0:T(8,128)S(1)}, u32[]{:S(2)}, u32[]{:S(2)}) async-start(f32[4,9,2,8,128]{4,3,2,1,0:T(8,128)} %smooth.1), calls=%async_computation.1 | async-start | bytes 589824 | tf_op jit(solution)/shard_map/all_to_all | solution.py:325
  44.1 5.5 %all-to-all-done.1 = f32[4,9,2,8,128]{4,3,2,1,0:T(8,128)S(1)} async-done(((f32[4,9,2,8,128]{4,3,2,1,0:T(8,128)}), f32[4,9,2,8,128]{4,3,2,1,0:T(8,128)S(1)}, u32[]{:S(2)}, u32[]{:S(2)}) %all-to-all-start.1) | async-done | bytes 294944 | tf_op jit(solution)/shard_map/all_to_all | solution.py:325
  49.9 38.7 %all_to_all.35 = bf16[128,2,512]{2,1,0:T(2,128)(2,1)S(1)} all-to-all(bf16[128,2,512]{2,1,0:T(2,128)(2,1)S(1)} %bitcast.52), channel_id=1, replica_groups=mesh['lon_0'=4,'lon_1'=2,'lat'=16,'lev'=4] {'lon_0','lon_1','lat'}, dimensions={0} | all-to-all | bytes 524288 | tf_op jit(solution)/shard_map/all_to_all | solution.py:410
  88.7 1.7 fusion.2
  92.1 1.6 fusion
  94.0 28.6 %all_to_all.36 = bf16[128,2,512]{2,1,0:T(2,128)(2,1)S(1)} all-to-all(bf16[128,2,512]{2,1,0:T(2,128)(2,1)S(1)} %bitcast.55), channel_id=1, replica_groups=mesh['lon_0'=4,'lon_1'=2,'lat'=16,'lev'=4] {'lon_0','lon_1','lat'}, dimensions={0} | all-to-all | bytes 524288 | tf_op jit(solution)/shard_map/all_to_all | solution.py:418
  123.0 10.1 %all_to_all.37.own_ref.pair_ref = bf16[4,18,2,8,128]{4,3,2,1,0:T(8,128)(2,1)S(1)} all-to-all(bf16[4,18,2,8,128]{4,3,2,1,0:T(8,128)(2,1)S(1)} %back.1), channel_id=1, replica_groups=mesh['lon_0'=4,'lon_1'=2,'lat'=16,'lev'=4] {'lev'}, dimensions={0} | all-to-all | bytes 589824 | tf_op jit(solution)/shard_map/all_to_all | solution.py:325
  133.1 2.1 %collective-permute-start.4 = (bf16[4,9,8,128]{3,2,1,0:T(8,128)(2,1)S(1)}, bf16[4,9,8,128]{3,2,1,0:T(8,128)(2,1)S(1)}, u32[]{:S(2)}, u32[]{:S(2)}) collective-permute-start(bf16[4,9,8,128]{3,2,1,0:T(8,128)(2,1)S(1)} %bitcast.60), channel_id=1, source_target_pairs={{0,4},{4,8},{8,12},{12,16},{16,20},{20,24},{24,28},{28,32},{32,36}... | collective-permute-start | bytes 221192 | tf_op jit(solution)/shard_map/ppermute | solution.py:26
  135.2 4.4 %collective-permute-start.5 = (bf16[4,9,8,128]{3,2,1,0:T(8,128)(2,1)S(1)}, bf16[4,9,8,128]{3,2,1,0:T(8,128)(2,1)S(1)}, u32[]{:S(2)}, u32[]{:S(2)}) collective-permute-start(bf16[4,9,8,128]{3,2,1,0:T(8,128)(2,1)S(1)} %bitcast.59), channel_id=1, source_target_pairs={{0,60},{4,0},{8,4},{12,8},{16,12},{20,16},{24,20},{28,24},{32,28},... | collective-permute-start | bytes 221192 | tf_op jit(solution)/shard_map/ppermute | solution.py:26
  139.6 1.4 collective-permute-done.5.south_ref
  141.3 2.0 %collective-permute-start.7 = (f32[9,8,128]{2,1,0:T(8,128)S(1)}, f32[9,8,128]{2,1,0:T(8,128)S(1)}, u32[]{:S(2)}, u32[]{:S(2)}) collective-permute-start(f32[9,8,128]{2,1,0:T(8,128)S(1)} %get-tuple-element.16.first_ref), channel_id=1, source_target_pairs={{0,448},{64,0},{128,64},{192,128},{256,192},{320,256},{384,320},{4... | collective-permute-start | bytes 110600 | tf_op jit(solution)/shard_map/ppermute | solution.py:26
  143.4 1.6 collective-permute-done.7.east_ref
  145.0 4.0 %image.1 = f32[4,10,2,8,128]{4,3,2,1,0:T(8,128)S(1)} custom-call(s32[2]{0:T(128)S(1)} %pad_add_fusion.place_ref, f32[4,9,2,16,128]{4,3,2,1,0:T(8,128)S(1)} %get-tuple-element.15.full_ref, f32[9,8,128]{2,1,0:T(8,128)S(1)} %get-tuple-element.16.first_ref, f32[9,8,128]{2,1,0:T(8,128)S(1)} %get-tuple-element.17.last_ref, ...), custom_call_target="tpu_custom_call" | custom-call | tf_op jit(solution)/shard_map/image/pallas_call | solution.py:332
  149.0 8.2 %all_to_all.38.image_ref = f32[4,10,2,8,128]{4,3,2,1,0:T(8,128)S(1)} all-to-all(f32[4,10,2,8,128]{4,3,2,1,0:T(8,128)S(1)} %image.1), channel_id=1, replica_groups=mesh['lon_0'=4,'lon_1'=2,'lat'=16,'lev'=4] {'lev'}, dimensions={0} | all-to-all | bytes 655360 | tf_op jit(solution)/shard_map/all_to_all | solution.py:325
  157.3 26.8 %all_to_all.39 = f32[128,1,128]{2,1,0:T(1,128)S(1)} all-to-all(f32[128,1,128]{2,1,0:T(1,128)S(1)} %broadcast_in_dim.21), channel_id=1, replica_groups=mesh['lon_0'=4,'lon_1'=2,'lat'=16,'lev'=4] {'lon_0','lon_1','lat'}, dimensions={0} | all-to-all | bytes 131072 | tf_op jit(solution)/shard_map/all_to_all | solution.py:429
  184.1 1.1 update.1
  (48 shorter events, 10.8 us)
Async XLA Ops:
  0.6 88.0 %copy-start = (bf16[1,1,1,128,2,8,512]{6,5,4,3,2,1,0:T(8,128)(2,1)S(1)}, bf16[1,1,1,128,2,8,512]{6,5,4,3,2,1,0:T(8,128)(2,1)}, u32[]{:S(2)}) copy-start(bf16[1,1,1,128,2,8,512]{6,5,4,3,2,1,0:T(8,128)(2,1)} %param.16) | copy-start | bytes 6291460
  0.6 49.0 %copy-start.1 = (bf16[32,4,2,8,128]{4,3,2,1,0:T(8,128)(2,1)S(1)}, bf16[32,4,2,8,128]{4,3,2,1,0:T(8,128)(2,1)}, u32[]{:S(2)}) copy-start(bf16[32,4,2,8,128]{4,3,2,1,0:T(8,128)(2,1)} %ensemble_ref.3) | copy-start | bytes 1572868
  0.7 48.9 %copy-start.5 = (f32[4,2,8,128]{3,2,1,0:T(8,128)S(1)}, f32[4,2,8,128]{3,2,1,0:T(8,128)}, u32[]{:S(2)}) copy-start(f32[4,2,8,128]{3,2,1,0:T(8,128)} %static_sd_ref.3) | copy-start | bytes 98308
  0.7 10.8 %all-to-all-start = ((f32[4,9,2,8,128]{4,3,2,1,0:T(8,128)}), f32[4,9,2,8,128]{4,3,2,1,0:T(8,128)S(1)}, u32[]{:S(2)}, u32[]{:S(2)}) async-start(f32[4,9,2,8,128]{4,3,2,1,0:T(8,128)} %bitcast.48), calls=%async_computation | async-start | bytes 589824 | tf_op jit(solution)/shard_map/all_to_all | solution.py:325
  11.6 14.1 %collective-permute-start = (bf16[4,9,8,128]{3,2,1,0:T(8,128)(2,1)S(1)}, bf16[4,9,8,128]{3,2,1,0:T(8,128)(2,1)S(1)}, u32[]{:S(2)}, u32[]{:S(2)}) collective-permute-start(bf16[4,9,8,128]{3,2,1,0:T(8,128)(2,1)S(1)} %bitcast.58), channel_id=1, source_target_pairs={{0,4},{4,8},{8,12},{12,16},{16,20},{20,24},{24,28},{28,32},{32,36}... | collective-permute-start | bytes 221192 | tf_op jit(solution)/shard_map/ppermute | solution.py:26
  15.3 11.0 %collective-permute-start.1 = (bf16[4,9,8,128]{3,2,1,0:T(8,128)(2,1)S(1)}, bf16[4,9,8,128]{3,2,1,0:T(8,128)(2,1)S(1)}, u32[]{:S(2)}, u32[]{:S(2)}) collective-permute-start(bf16[4,9,8,128]{3,2,1,0:T(8,128)(2,1)S(1)} %bitcast.57), channel_id=1, source_target_pairs={{0,60},{4,0},{8,4},{12,8},{16,12},{20,16},{24,20},{28,24},{32,28},... | collective-permute-start | bytes 221192 | tf_op jit(solution)/shard_map/ppermute | solution.py:26
  25.7 0.6 copy-start.6
  26.3 0.6 copy-start.8
  26.9 0.9 copy-start.7
  27.8 0.9 copy-start.9
  29.7 5.9 %collective-permute-start.3 = (f32[9,8,128]{2,1,0:T(8,128)}, f32[9,8,128]{2,1,0:T(8,128)}, u32[]{:S(2)}, u32[]{:S(2)}) collective-permute-start(f32[9,8,128]{2,1,0:T(8,128)} %get-tuple-element.13.first_ref), channel_id=1, source_target_pairs={{0,448},{64,0},{128,64},{192,128},{256,192},{320,256},{384,320},{4... | collective-permute-start | bytes 110600 | tf_op jit(solution)/shard_map/ppermute | solution.py:26
  32.6 3.1 %collective-permute-start.2 = (f32[9,8,128]{2,1,0:T(8,128)}, f32[9,8,128]{2,1,0:T(8,128)}, u32[]{:S(2)}, u32[]{:S(2)}) collective-permute-start(f32[9,8,128]{2,1,0:T(8,128)} %get-tuple-element.14.last_ref), channel_id=1, source_target_pairs={{0,64},{64,128},{128,192},{192,256},{256,320},{320,384},{384,448},... | collective-permute-start | bytes 110600 | tf_op jit(solution)/shard_map/ppermute | solution.py:26
  40.5 9.1 %all-to-all-start.1 = ((f32[4,9,2,8,128]{4,3,2,1,0:T(8,128)}), f32[4,9,2,8,128]{4,3,2,1,0:T(8,128)S(1)}, u32[]{:S(2)}, u32[]{:S(2)}) async-start(f32[4,9,2,8,128]{4,3,2,1,0:T(8,128)} %smooth.1), calls=%async_computation.1 | async-start | bytes 589824 | tf_op jit(solution)/shard_map/all_to_all | solution.py:325
  88.7 2.6 %copy-start.10 = (f32[1,1,1,128,2,8]{3,5,4,2,1,0:T(8,128)S(1)}, f32[1,1,1,128,2,8]{3,5,4,2,1,0:T(8,128)}, u32[]{:S(2)}) copy-start(f32[1,1,1,128,2,8]{3,5,4,2,1,0:T(8,128)} %param.17) | copy-start | bytes 24580
  91.3 31.3 %copy-start.2 = (f32[36,2,8,128]{3,2,1,0:T(8,128)S(1)}, f32[36,2,8,128]{3,2,1,0:T(8,128)}, u32[]{:S(2)}) copy-start(f32[36,2,8,128]{3,2,1,0:T(8,128)} %residual_ref.1) | copy-start | bytes 884740
  123.0 61.1 %copy-start.3 = (f32[36,2,8,128]{3,2,1,0:T(8,128)S(1)}, f32[36,2,8,128]{3,2,1,0:T(8,128)}, u32[]{:S(2)}) copy-start(f32[36,2,8,128]{3,2,1,0:T(8,128)} %param.11) | copy-start | bytes 884740
  123.0 61.1 %copy-start.4 = (f32[36,2,8,128]{3,2,1,0:T(8,128)S(1)}, f32[36,2,8,128]{3,2,1,0:T(8,128)}, u32[]{:S(2)}) copy-start(f32[36,2,8,128]{3,2,1,0:T(8,128)} %param.9) | copy-start | bytes 884740
  133.1 6.5 %collective-permute-start.4 = (bf16[4,9,8,128]{3,2,1,0:T(8,128)(2,1)S(1)}, bf16[4,9,8,128]{3,2,1,0:T(8,128)(2,1)S(1)}, u32[]{:S(2)}, u32[]{:S(2)}) collective-permute-start(bf16[4,9,8,128]{3,2,1,0:T(8,128)(2,1)S(1)} %bitcast.60), channel_id=1, source_target_pairs={{0,4},{4,8},{8,12},{12,16},{16,20},{20,24},{24,28},{28,32},{32,36}... | collective-permute-start | bytes 221192 | tf_op jit(solution)/shard_map/ppermute | solution.py:26
  135.2 5.8 %collective-permute-start.5 = (bf16[4,9,8,128]{3,2,1,0:T(8,128)(2,1)S(1)}, bf16[4,9,8,128]{3,2,1,0:T(8,128)(2,1)S(1)}, u32[]{:S(2)}, u32[]{:S(2)}) collective-permute-start(bf16[4,9,8,128]{3,2,1,0:T(8,128)(2,1)S(1)} %bitcast.59), channel_id=1, source_target_pairs={{0,60},{4,0},{8,4},{12,8},{16,12},{20,16},{24,20},{28,24},{32,28},... | collective-permute-start | bytes 221192 | tf_op jit(solution)/shard_map/ppermute | solution.py:26
  141.3 3.7 %collective-permute-start.7 = (f32[9,8,128]{2,1,0:T(8,128)S(1)}, f32[9,8,128]{2,1,0:T(8,128)S(1)}, u32[]{:S(2)}, u32[]{:S(2)}) collective-permute-start(f32[9,8,128]{2,1,0:T(8,128)S(1)} %get-tuple-element.16.first_ref), channel_id=1, source_target_pairs={{0,448},{64,0},{128,64},{192,128},{256,192},{320,256},{384,320},{4... | collective-permute-start | bytes 110600 | tf_op jit(solution)/shard_map/ppermute | solution.py:26
  143.3 1.7 collective-permute-start.6

commit v5 on v3

--- a/solution.py
+++ b/solution.py
@@ -91,6 +91,11 @@
         if step < 3:
             left, right = one_pass(left), one_pass(right)
     near_ref[...] = near
+
+
+lat_ratio = spread_lat / spread_lon
+assert spread_lev == spread_lon
+centre_ratio = centre_part / spread_lon
 
 
 def field_passes(coefficients, x, near, far):
@@ -112,7 +117,6 @@
             )
             for h in range(2):
                 here = x[2 * p + h]
-                centre, lon_part, lat_part, lev_part = coefficients[h]
                 start = (2 * p + h) * 8
                 edge = edges[start : start + 8]
                 if step:
@@ -120,13 +124,14 @@
                 beside = jnp.where(left_edge, edge, pltpu.roll(here, 1, 1)) + jnp.where(
                     right_edge, edge, pltpu.roll(here, 127, 1)
                 )
-                total = centre * here + lon_part * beside + lat_part * across[h]
                 if p == 0:
-                    total = total + lev_part * x[2 + h]
+                    beside = beside + x[2 + h]
                 elif p == planes - 1:
-                    total = total + lev_part * x[2 * p - 2 + h]
+                    beside = beside + x[2 * p - 2 + h]
                 else:
-                    total = total + lev_part * (x[2 * p - 2 + h] + x[2 * p + 2 + h])
+                    beside = beside + (x[2 * p - 2 + h] + x[2 * p + 2 + h])
+                total = beside + lat_ratio * across[h]
+                total = coefficients[h] * (total + centre_ratio * here)
                 result.append(total)
         x = result
     return x
@@ -139,9 +144,7 @@
         low = jnp.where(place_ref[0] == 0, HALO, 0)
         high = jnp.where(place_ref[0] == place_ref[1] - 1, 16 - HALO, 16)
         inside = jnp.where((row >= low) & (row < high), 1.0, 0.0).astype(jnp.float32)
-        halves.append(
-            (inside * centre_part, inside * spread_lon, inside * spread_lat, inside * spread_lev)
-        )
+        halves.append(inside * spread_lon)
     return halves
 
 
@@ -387,8 +390,6 @@
     groups = lax.axis_size("lev")
     share = direction.shape[0] // groups
     grouped = (groups, share, levels, lat_rows, lon_cells)
-    direction_blocks = swap_lev(direction.reshape(grouped))
-    smoothed = swap_lev(smooth(direction_blocks, share)).reshape(direction.shape)
     tile_pick = send_tile.reshape(group_size, 1, slot_count)
     is_live = (
         jnp.arange(slot_count, dtype=jnp.int32)[None, :] < pair_count.reshape(group_size)[:, None]
@@ -398,6 +399,9 @@
     row_pick = row_pick.reshape(group_size * variables * slot_count)
     chosen = row_pick[:, None] == jnp.arange(variables * tile_total, dtype=jnp.int32)[None, :]
     chosen = chosen.astype(jnp.bfloat16)
+    direction_blocks = swap_lev(direction.reshape(grouped))
+    direction_blocks, chosen = lax.optimization_barrier((direction_blocks, chosen))
+    smoothed = swap_lev(smooth(direction_blocks, share)).reshape(direction.shape)
     scales = (scale_ens, static_part)
     rows = jax.ShapeDtypeStruct((group_size * variables * slot_count, lon_cells), jnp.bfloat16)
     outgoing = local_call(functools.partial(tiles_kernel, scales), rows, 0, "tiles")(

time: 187 us -> 184 us (0.984)
  blocking collectives: 116 us -> 123 us
  waiting for transfers between devices: 15.7 us -> 11.6 us
  starting transfers between devices: 34.2 us -> 30.8 us
    all_to_all x2 -> x3, blocking collectives: 21.3 us -> 29.4 us  [swap_lev(): lax.all_to_all(blocks, 'lev', split_axis=0, concat_axis=0, tiled=True)]
    all_to_all x2 -> x1, waiting for transfers between devices: 9.63 us -> 3.57 us  [swap_lev(): lax.all_to_all(blocks, 'lev', split_axis=0, concat_axis=0, tiled=True)]
    all_to_all x2 -> x1, starting transfers between devices: 8.6 us -> 5.14 us  [swap_lev(): lax.all_to_all(blocks, 'lev', split_axis=0, concat_axis=0, tiled=True)]
    ppermute x8, waiting for transfers between devices: 6.06 us -> 8.07 us  [shift(): lax.ppermute(x, axis, [(i, (i + step) % devices) for i in range(devices)])]
  transfers between devices with their start and end apart: 10 -> 9, of which waited for: 7 -> 7; matrix products, arithmetic and copies ran while one was open for 2% -> 1% of each run, Pallas kernels for 0% -> 0%
where the time goes in v5:
time: 184 us
  blocking collectives  123 us (67%)
  starting transfers between devices  30.8 us (17%)
  waiting for transfers between devices  11.6 us (6%)
  Pallas kernels  10.3 us (6%)
  local copies, waits for them, and re-layouts  3.08 us (2%)
  matrix products  2.57 us (1%)
    all_to_all x1, blocking collectives, body(): lax.all_to_all(outgoing, LON_LAT, split_axis=0, concat_axis=0, tiled=True)  38.7 us
    all_to_all x3, blocking collectives, swap_lev(): lax.all_to_all(blocks, 'lev', split_axis=0, concat_axis=0, tiled=True)  29.4 us
    all_to_all x1, blocking collectives, body(): lax.all_to_all(returned, LON_LAT, split_axis=0, concat_axis=0, tiled=True)  28.6 us
    all_to_all x1, blocking collectives, body(): lax.all_to_all(jnp.broadcast_to(row, (peers, 1, lon_cells)), LON_LAT, spl...  26.7 us
    ppermute x8, starting transfers between devices, shift(): lax.ppermute(x, axis, [(i, (i + step) % devices) for i in range(devices)])  25.7 us
    pallas_call x7, Pallas kernels, run(): pl.pallas_call(kernel, out_shape=out_shape, in_specs=in_specs, out_specs=...  10.3 us
    ppermute x8, waiting for transfers between devices, shift(): lax.ppermute(x, axis, [(i, (i + step) % devices) for i in range(devices)])  8.07 us
    all_to_all x1, starting transfers between devices, swap_lev(): lax.all_to_all(blocks, 'lev', split_axis=0, concat_axis=0, tiled=True)  5.14 us
  transfers between devices with their start and end apart: 9, of which 7 were waited for; matrix products, arithmetic and copies ran while one was open for 1% of the time, Pallas kernels for 0%

profile of v5, /device:TPU:1, one launch (start us, length us, event | category | flops | bytes accessed | tf_op | source)
XLA Modules:
  0.0 183.8 jit_solution(1340598770821271189)
XLA Ops:
  0.7 5.1 %all-to-all-start = ((f32[4,9,2,8,128]{4,3,2,1,0:T(8,128)}), f32[4,9,2,8,128]{4,3,2,1,0:T(8,128)S(1)}, u32[]{:S(2)}, u32[]{:S(2)}) async-start(f32[4,9,2,8,128]{4,3,2,1,0:T(8,128)} %bitcast.47), calls=%async_computation | async-start | bytes 589824 | tf_op jit(solution)/shard_map/all_to_all | solution.py:327
  8.0 3.6 %all-to-all-done.own_ref.direction_ref = f32[4,9,2,8,128]{4,3,2,1,0:T(8,128)S(1)} async-done(((f32[4,9,2,8,128]{4,3,2,1,0:T(8,128)}), f32[4,9,2,8,128]{4,3,2,1,0:T(8,128)S(1)}, u32[]{:S(2)}, u32[]{:S(2)}) %all-to-all-start) | async-done | bytes 294944 | tf_op jit(solution)/shard_map/all_to_all | solution.py:327
  12.3 3.7 %collective-permute-start = (f32[4,9,8,128]{3,2,1,0:T(8,128)}, f32[4,9,8,128]{3,2,1,0:T(8,128)S(1)}, u32[]{:S(2)}, u32[]{:S(2)}) collective-permute-start(f32[4,9,8,128]{3,2,1,0:T(8,128)} %bitcast.5), channel_id=1, source_target_pairs={{0,4},{4,8},{8,12},{12,16},{16,20},{20,24},{24,28},{28,32},{32,36}... | collective-permute-start | bytes 442376 | tf_op jit(solution)/shard_map/ppermute | solution.py:26
  16.0 9.5 %collective-permute-start.1 = (f32[4,9,8,128]{3,2,1,0:T(8,128)}, f32[4,9,8,128]{3,2,1,0:T(8,128)S(1)}, u32[]{:S(2)}, u32[]{:S(2)}) collective-permute-start(f32[4,9,8,128]{3,2,1,0:T(8,128)} %bitcast.6), channel_id=1, source_target_pairs={{0,60},{4,0},{8,4},{12,8},{16,12},{20,16},{24,20},{28,24},{32,28},... | collective-permute-start | bytes 442376 | tf_op jit(solution)/shard_map/ppermute | solution.py:26
  26.3 1.6 collective-permute-done.1.south_ref
  28.3 3.0 %collective-permute-start.3 = (f32[9,8,128]{2,1,0:T(8,128)S(1)}, f32[9,8,128]{2,1,0:T(8,128)S(1)}, u32[]{:S(2)}, u32[]{:S(2)}) collective-permute-start(f32[9,8,128]{2,1,0:T(8,128)S(1)} %get-tuple-element.16.first_ref), channel_id=1, source_target_pairs={{0,448},{64,0},{128,64},{192,128},{256,192},{320,256},{384,320},{4... | collective-permute-start | bytes 110600 | tf_op jit(solution)/shard_map/ppermute | solution.py:26
  31.3 1.1 collective-permute-start.2
  32.4 1.5 collective-permute-done.3.east_ref
  34.0 3.8 %smooth.1 = f32[4,9,2,8,128]{4,3,2,1,0:T(8,128)S(1)} custom-call(s32[2]{0:T(128)S(1)} %pad_add_fusion.place_ref, f32[4,9,2,16,128]{4,3,2,1,0:T(8,128)S(1)} %get-tuple-element.15.full_ref, f32[9,8,128]{2,1,0:T(8,128)S(1)} %get-tuple-element.16.first_ref, f32[9,8,128]{2,1,0:T(8,128)S(1)} %get-tuple-element.17.last_ref, ...), custom_call_target="tpu_custom_call" | custom-call | tf_op jit(solution)/shard_map/smooth/pallas_call | solution.py:334
  37.8 8.1 %all_to_all.35 = f32[4,9,2,8,128]{4,3,2,1,0:T(8,128)S(1)} all-to-all(f32[4,9,2,8,128]{4,3,2,1,0:T(8,128)S(1)} %smooth.1), channel_id=1, replica_groups=mesh['lon_0'=4,'lon_1'=2,'lat'=16,'lev'=4] {'lev'}, dimensions={0} | all-to-all | bytes 589824 | tf_op jit(solution)/shard_map/all_to_all | solution.py:327
  46.2 38.7 %all_to_all.36 = bf16[128,2,512]{2,1,0:T(2,128)(2,1)S(1)} all-to-all(bf16[128,2,512]{2,1,0:T(2,128)(2,1)S(1)} %bitcast.52), channel_id=1, replica_groups=mesh['lon_0'=4,'lon_1'=2,'lat'=16,'lev'=4] {'lon_0','lon_1','lat'}, dimensions={0} | all-to-all | bytes 524288 | tf_op jit(solution)/shard_map/all_to_all | solution.py:413
  84.9 1.0 fusion.2
  86.8 1.6 fusion
  88.7 28.6 %all_to_all.37 = bf16[128,2,512]{2,1,0:T(2,128)(2,1)S(1)} all-to-all(bf16[128,2,512]{2,1,0:T(2,128)(2,1)S(1)} %bitcast.55), channel_id=1, replica_groups=mesh['lon_0'=4,'lon_1'=2,'lat'=16,'lev'=4] {'lon_0','lon_1','lat'}, dimensions={0} | all-to-all | bytes 524288 | tf_op jit(solution)/shard_map/all_to_all | solution.py:421
  117.6 13.1 %all_to_all.38.own_ref.pair_ref = f32[4,18,2,8,128]{4,3,2,1,0:T(8,128)S(1)} all-to-all(f32[4,18,2,8,128]{4,3,2,1,0:T(8,128)S(1)} %back.1), channel_id=1, replica_groups=mesh['lon_0'=4,'lon_1'=2,'lat'=16,'lev'=4] {'lev'}, dimensions={0} | all-to-all | bytes 1179648 | tf_op jit(solution)/shard_map/all_to_all | solution.py:327
  130.8 2.5 %collective-permute-start.4 = (f32[4,9,8,128]{3,2,1,0:T(8,128)S(1)}, f32[4,9,8,128]{3,2,1,0:T(8,128)S(1)}, u32[]{:S(2)}, u32[]{:S(2)}) collective-permute-start(f32[4,9,8,128]{3,2,1,0:T(8,128)S(1)} %bitcast.58), channel_id=1, source_target_pairs={{0,4},{4,8},{8,12},{12,16},{16,20},{20,24},{24,28},{28,32},{32,36}... | collective-permute-start | bytes 442376 | tf_op jit(solution)/shard_map/ppermute | solution.py:26
  133.3 4.1 %collective-permute-start.5 = (f32[4,9,8,128]{3,2,1,0:T(8,128)S(1)}, f32[4,9,8,128]{3,2,1,0:T(8,128)S(1)}, u32[]{:S(2)}, u32[]{:S(2)}) collective-permute-start(f32[4,9,8,128]{3,2,1,0:T(8,128)S(1)} %bitcast.57), channel_id=1, source_target_pairs={{0,60},{4,0},{8,4},{12,8},{16,12},{20,16},{24,20},{28,24},{32,28},... | collective-permute-start | bytes 442376 | tf_op jit(solution)/shard_map/ppermute | solution.py:26
  137.4 1.6 collective-permute-done.4.north_ref
  140.3 1.6 collective-permute-start.7
  142.1 1.6 collective-permute-done.7.east_ref
  143.7 3.9 %image.1 = f32[4,10,2,8,128]{4,3,2,1,0:T(8,128)S(1)} custom-call(s32[2]{0:T(128)S(1)} %pad_add_fusion.place_ref, f32[4,9,2,16,128]{4,3,2,1,0:T(8,128)S(1)} %get-tuple-element.19.full_ref, f32[9,8,128]{2,1,0:T(8,128)S(1)} %get-tuple-element.20.first_ref, f32[9,8,128]{2,1,0:T(8,128)S(1)} %get-tuple-element.21.last_ref, ...), custom_call_target="tpu_custom_call" | custom-call | tf_op jit(solution)/shard_map/image/pallas_call | solution.py:334
  147.7 8.2 %all_to_all.39.image_ref = f32[4,10,2,8,128]{4,3,2,1,0:T(8,128)S(1)} all-to-all(f32[4,10,2,8,128]{4,3,2,1,0:T(8,128)S(1)} %image.1), channel_id=1, replica_groups=mesh['lon_0'=4,'lon_1'=2,'lat'=16,'lev'=4] {'lev'}, dimensions={0} | all-to-all | bytes 655360 | tf_op jit(solution)/shard_map/all_to_all | solution.py:327
  156.0 26.7 %all_to_all.40 = f32[128,1,128]{2,1,0:T(1,128)S(1)} all-to-all(f32[128,1,128]{2,1,0:T(1,128)S(1)} %broadcast_in_dim.21), channel_id=1, replica_groups=mesh['lon_0'=4,'lon_1'=2,'lat'=16,'lev'=4] {'lon_0','lon_1','lat'}, dimensions={0} | all-to-all | bytes 131072 | tf_op jit(solution)/shard_map/all_to_all | solution.py:432
  182.7 1.1 update.1
  (38 shorter events, 7.6 us)
Async XLA Ops:
  0.6 84.2 %copy-start = (bf16[1,1,1,128,2,8,512]{6,5,4,3,2,1,0:T(8,128)(2,1)S(1)}, bf16[1,1,1,128,2,8,512]{6,5,4,3,2,1,0:T(8,128)(2,1)}, u32[]{:S(2)}) copy-start(bf16[1,1,1,128,2,8,512]{6,5,4,3,2,1,0:T(8,128)(2,1)} %param.16) | copy-start | bytes 6291460
  0.6 45.2 %copy-start.1 = (bf16[32,4,2,8,128]{4,3,2,1,0:T(8,128)(2,1)S(1)}, bf16[32,4,2,8,128]{4,3,2,1,0:T(8,128)(2,1)}, u32[]{:S(2)}) copy-start(bf16[32,4,2,8,128]{4,3,2,1,0:T(8,128)(2,1)} %ensemble_ref.3) | copy-start | bytes 1572868
  0.7 45.2 %copy-start.5 = (f32[4,2,8,128]{3,2,1,0:T(8,128)S(1)}, f32[4,2,8,128]{3,2,1,0:T(8,128)}, u32[]{:S(2)}) copy-start(f32[4,2,8,128]{3,2,1,0:T(8,128)} %static_sd_ref.3) | copy-start | bytes 98308
  0.7 10.8 %all-to-all-start = ((f32[4,9,2,8,128]{4,3,2,1,0:T(8,128)}), f32[4,9,2,8,128]{4,3,2,1,0:T(8,128)S(1)}, u32[]{:S(2)}, u32[]{:S(2)}) async-start(f32[4,9,2,8,128]{4,3,2,1,0:T(8,128)} %bitcast.47), calls=%async_computation | async-start | bytes 589824 | tf_op jit(solution)/shard_map/all_to_all | solution.py:327
  12.3 14.0 %collective-permute-start = (f32[4,9,8,128]{3,2,1,0:T(8,128)}, f32[4,9,8,128]{3,2,1,0:T(8,128)S(1)}, u32[]{:S(2)}, u32[]{:S(2)}) collective-permute-start(f32[4,9,8,128]{3,2,1,0:T(8,128)} %bitcast.5), channel_id=1, source_target_pairs={{0,4},{4,8},{8,12},{12,16},{16,20},{20,24},{24,28},{28,32},{32,36}... | collective-permute-start | bytes 442376 | tf_op jit(solution)/shard_map/ppermute | solution.py:26
  16.0 11.9 %collective-permute-start.1 = (f32[4,9,8,128]{3,2,1,0:T(8,128)}, f32[4,9,8,128]{3,2,1,0:T(8,128)S(1)}, u32[]{:S(2)}, u32[]{:S(2)}) collective-permute-start(f32[4,9,8,128]{3,2,1,0:T(8,128)} %bitcast.6), channel_id=1, source_target_pairs={{0,60},{4,0},{8,4},{12,8},{16,12},{20,16},{24,20},{28,24},{32,28},... | collective-permute-start | bytes 442376 | tf_op jit(solution)/shard_map/ppermute | solution.py:26
  28.3 5.7 %collective-permute-start.3 = (f32[9,8,128]{2,1,0:T(8,128)S(1)}, f32[9,8,128]{2,1,0:T(8,128)S(1)}, u32[]{:S(2)}, u32[]{:S(2)}) collective-permute-start(f32[9,8,128]{2,1,0:T(8,128)S(1)} %get-tuple-element.16.first_ref), channel_id=1, source_target_pairs={{0,448},{64,0},{128,64},{192,128},{256,192},{320,256},{384,320},{4... | collective-permute-start | bytes 110600 | tf_op jit(solution)/shard_map/ppermute | solution.py:26
  31.3 2.7 %collective-permute-start.2 = (f32[9,8,128]{2,1,0:T(8,128)S(1)}, f32[9,8,128]{2,1,0:T(8,128)S(1)}, u32[]{:S(2)}, u32[]{:S(2)}) collective-permute-start(f32[9,8,128]{2,1,0:T(8,128)S(1)} %get-tuple-element.17.last_ref), channel_id=1, source_target_pairs={{0,64},{64,128},{128,192},{192,256},{256,320},{320,384},{384,448},... | collective-permute-start | bytes 110600 | tf_op jit(solution)/shard_map/ppermute | solution.py:26
  84.9 1.1 copy-start.6
  85.9 31.3 %copy-start.3 = (f32[36,2,8,128]{3,2,1,0:T(8,128)S(1)}, f32[36,2,8,128]{3,2,1,0:T(8,128)}, u32[]{:S(2)}) copy-start(f32[36,2,8,128]{3,2,1,0:T(8,128)} %residual_ref.1) | copy-start | bytes 884740
  130.7 52.0 %copy-start.2 = (f32[36,2,8,128]{3,2,1,0:T(8,128)S(1)}, f32[36,2,8,128]{3,2,1,0:T(8,128)}, u32[]{:S(2)}) copy-start(f32[36,2,8,128]{3,2,1,0:T(8,128)} %param.11) | copy-start | bytes 884740
  130.7 52.0 %copy-start.4 = (f32[36,2,8,128]{3,2,1,0:T(8,128)S(1)}, f32[36,2,8,128]{3,2,1,0:T(8,128)}, u32[]{:S(2)}) copy-start(f32[36,2,8,128]{3,2,1,0:T(8,128)} %param.9) | copy-start | bytes 884740
  130.8 8.2 %collective-permute-start.4 = (f32[4,9,8,128]{3,2,1,0:T(8,128)S(1)}, f32[4,9,8,128]{3,2,1,0:T(8,128)S(1)}, u32[]{:S(2)}, u32[]{:S(2)}) collective-permute-start(f32[4,9,8,128]{3,2,1,0:T(8,128)S(1)} %bitcast.58), channel_id=1, source_target_pairs={{0,4},{4,8},{8,12},{12,16},{16,20},{20,24},{24,28},{28,32},{32,36}... | collective-permute-start | bytes 442376 | tf_op jit(solution)/shard_map/ppermute | solution.py:26
  133.3 6.6 %collective-permute-start.5 = (f32[4,9,8,128]{3,2,1,0:T(8,128)S(1)}, f32[4,9,8,128]{3,2,1,0:T(8,128)S(1)}, u32[]{:S(2)}, u32[]{:S(2)}) collective-permute-start(f32[4,9,8,128]{3,2,1,0:T(8,128)S(1)} %bitcast.57), channel_id=1, source_target_pairs={{0,60},{4,0},{8,4},{12,8},{16,12},{20,16},{24,20},{28,24},{32,28},... | collective-permute-start | bytes 442376 | tf_op jit(solution)/shard_map/ppermute | solution.py:26
  140.3 3.4 %collective-permute-start.7 = (f32[9,8,128]{2,1,0:T(8,128)S(1)}, f32[9,8,128]{2,1,0:T(8,128)S(1)}, u32[]{:S(2)}, u32[]{:S(2)}) collective-permute-start(f32[9,8,128]{2,1,0:T(8,128)S(1)} %get-tuple-element.20.first_ref), channel_id=1, source_target_pairs={{0,448},{64,0},{128,64},{192,128},{256,192},{320,256},{384,320},{4... | collective-permute-start | bytes 110600 | tf_op jit(solution)/shard_map/ppermute | solution.py:26
  142.0 1.8 collective-permute-start.6
